TPU v7x, 32 devices: a whole 2x2x4 slice. The times are simulated.
32 devices in a mesh: lat: 4 (over z), lon: 8 (over y, x, core).
Axes of the slice: x: 2, y: 2, z: 4, core: 2. Of those that a mesh axis runs over, the one named last changes fastest.
Arguments:
- fields: float32 [32, 2880, 384], P('lat', 'lon'), may hold values from -6 to 6
- cutoff: int32 [32], P('lat'), may hold values from 1 to 1395, as said below
Outputs:
- filtered: float32 [32, 2880, 384], P('lat', 'lon')
Inputs may be any that keep to these rules, and one draw needn't show every extreme that they name: cutoff[g] lies between 1 and 1 + (1439)(2 p + 1) // 32, where p is the number of rows between row g and the nearer pole; this ceiling grows from the pole rows to the equator.
All inputs are finite; a program needn't handle non-finite values.
Results may differ from a plain program's by a relative error of at most 0.0003.
Values sent between devices are 32-bit elements; how exact they have to be, the bound alone decides.
A program may use at most 64 MiB of HBM per device.

v0:
```python
import functools
import math

import jax
import jax.numpy as jnp
import ml_dtypes
import numpy as np
from jax import lax
from jax.experimental import pallas as pl
from jax.experimental.pallas import tpu as pltpu
from jax.sharding import PartitionSpec as P

RADIX = 8


def split_np(a):
    hi = a.astype(ml_dtypes.bfloat16)
    lo = (a - hi.astype(np.float64)).astype(ml_dtypes.bfloat16)
    return hi, lo


def fourier_table(sub, padded):
    turn = np.outer(np.arange(sub), np.arange(sub)) % sub
    angle = 2.0 * np.pi * turn / sub
    both = np.concatenate([np.cos(angle), np.sin(angle)], axis=0)
    both = np.pad(both, ((0, 0), (0, padded - sub)))
    hi, lo = split_np(both)
    return np.concatenate([hi, lo, hi], axis=1)


def twist_table(sub, length):
    b = np.arange(RADIX // 2 + 1)
    angle = 2.0 * np.pi * np.outer(np.arange(sub), b) / length
    return np.concatenate([np.cos(angle), np.sin(angle)], axis=1).astype(np.float32)


def gain_table(cut, sub, length):
    half = RADIX // 2
    wave = np.arange(sub)[:, None] * RADIX + np.arange(half + 1)[None, :]
    folded = np.minimum(wave, length - wave)
    scale = np.where((np.arange(half + 1) % half) == 0, 1.0, 2.0)[None, :] / length
    inverse_sine = 1.0 / np.sin(np.pi * np.maximum(folded, 1) / length)
    ratio = jnp.sin(cut * jnp.float32(math.pi / length)) * inverse_sine.astype(np.float32)
    gain = jnp.where(folded.astype(np.float32) <= cut, 1.0, ratio * ratio)
    return gain * scale.astype(np.float32)


def three(table, z, padded):
    pad = padded - z.shape[0]
    if pad:
        z = jnp.concatenate([z, jnp.zeros((pad, z.shape[1]), z.dtype)], axis=0)
    hi = z.astype(jnp.bfloat16)
    lo = (z - hi.astype(jnp.float32)).astype(jnp.bfloat16)
    return jnp.dot(table, jnp.concatenate([hi, hi, lo], axis=0), preferred_element_type=jnp.float32)


def filter_row(sub, padded, x_ref, table_ref, twist_ref, gains, y_ref):
    width = x_ref.shape[-1]
    half = RADIX // 2
    r = math.sqrt(0.5)
    x = [x_ref[pl.ds(j * sub, sub), :] for j in range(RADIX)]
    s = [x[j] + x[j + 4] for j in range(4)]
    d = [x[j] - x[j + 4] for j in range(4)]
    s02, s13 = s[0] + s[2], s[1] + s[3]
    p, q = r * (d[1] - d[3]), r * (d[1] + d[3])
    spectra = [
        (s02 + s13, None),
        (d[0] + p, -(d[2] + q)),
        (s[0] - s[2], s[3] - s[1]),
        (d[0] - p, d[2] - q),
        (s02 - s13, None),
    ]
    table = table_ref[...]
    back = []
    for b in range(half + 1):
        re, im = spectra[b]
        gain = gains[:, b : b + 1]
        if b == 0:
            f = three(table, re, padded)
            g = three(table, jnp.concatenate([f[:sub] * gain, f[sub:] * gain], axis=1), padded)
            back.append((g[:sub, :width] + g[sub:, width:], None))
            continue
        c = twist_ref[:, b : b + 1]
        t = twist_ref[:, half + 1 + b : half + 2 + b]
        if im is None:
            zr, zi = re * c, -(re * t)
        else:
            zr, zi = re * c + im * t, im * c - re * t
        f = three(table, jnp.concatenate([zr, zi], axis=1), padded)
        fr = (f[:sub, :width] + f[sub:, width:]) * gain
        fi = (f[:sub, width:] - f[sub:, :width]) * gain
        g = three(table, jnp.concatenate([fr, fi], axis=1), padded)
        gr = g[:sub, :width] - g[sub:, width:]
        gi = g[:sub, width:] + g[sub:, :width]
        back.append((gr * c - gi * t, gr * t + gi * c))
    y0, y4 = back[0][0], back[4][0]
    (a1, b1), (a2, b2), (a3, b3) = back[1:4]
    e, o = y0 + y4, y0 - y4
    u, v = a1 + a3, b1 - b3
    w, z = r * (a1 - a3), r * (b1 + b3)
    outs = {
        0: e + a2 + u,
        4: e + a2 - u,
        2: e - a2 - v,
        6: e - a2 + v,
        1: o - b2 + w - z,
        5: o - b2 - w + z,
        3: o + b2 - w - z,
        7: o + b2 + w + z,
    }
    for j in range(RADIX):
        y_ref[pl.ds(j * sub, sub), :] = outs[j]


def split_table(a):
    hi = a.astype(jnp.bfloat16)
    lo = (a - hi.astype(jnp.float32)).astype(jnp.bfloat16)
    return jnp.concatenate([hi, lo, hi], axis=1)


def snap(a):
    return (np.round(a * 2.0**22) / 2.0**22).astype(np.float32)


def toeplitz(symbol, sub):
    line = np.fft.ifft(symbol).real
    index = np.arange(sub)
    return line[(index[:, None] - index[None, :]) % symbol.shape[0]]


class Plan:
    def __init__(self, rows, segment, channels, ring, bands):
        length, total = segment * ring, rows * bands
        self.width = 128 if channels % 128 == 0 else channels
        blocks = channels // self.width
        row_ids = np.arange(total)
        polar = np.abs(2 * row_ids + 1 - total) * 5 > 2 * total
        poles = np.minimum(row_ids, total - 1 - row_ids)
        count = int(poles[polar].max()) + 1
        cuts = 1 + (length // 2 - 1) * (2 * np.arange(count) + 1) // total
        full = -(-segment // 8) * 8
        ranks = [min(full, -(-((2 * int(c) + 1) // ring + 21) // 8) * 8) for c in cuts]
        self.rank = max(ranks)
        self.rank_pad = -(-self.rank // 128) * 128
        self.sub_pad = -(-segment // 128) * 128
        wave = np.arange(length)
        folded = np.minimum(wave, length - wave)
        sine = np.sin(np.pi * np.maximum(folded, 1) / length) ** 2
        spot = np.arange(segment)
        probe = np.cos(1.0 + 0.37 * spot * spot)
        self.basis = np.zeros((count, segment, self.rank_pad), np.float32)
        self.basis_t = np.zeros((count, self.rank, self.sub_pad), np.float32)
        self.rest = np.zeros((count, segment, self.sub_pad), np.float32)
        top = np.sin(np.pi * cuts / length) ** 2
        self.top = top.astype(np.float32)
        for p in range(count):
            take = min(ranks[p], segment)
            side = spot[1:] * (segment - spot[1:]) / 2.0
            band = (cuts[p] + 0.5) / length
            tri = np.diag(((segment - 1) / 2.0 - spot) ** 2 * np.cos(2.0 * np.pi * band))
            tri = tri + np.diag(side, 1) + np.diag(side, -1)
            vectors = np.linalg.eigh(tri)[1][:, ::-1][:, :take]
            vectors = vectors * np.where(probe @ vectors < 0, -1.0, 1.0)
            basis = snap(vectors)
            if take == segment:
                basis = np.eye(segment, dtype=np.float32)
            self.basis[p, :, :take] = basis
            self.basis_t[p, :take, :segment] = basis.T
            near = toeplitz(np.minimum(1.0 / sine, 1.0 / top[p]) * top[p], segment)
            wide = basis.astype(np.float64)
            self.rest[p, :, :segment] = snap(near - wide @ (wide.T @ near @ wide) @ wide.T)
        slots = -(-rows * blocks // ring)
        self.slots = slots
        self.row_pole = np.zeros((bands, rows), np.int32)
        self.row_on = np.zeros((bands, rows), np.int32)
        self.dest = np.zeros((bands, rows, blocks), np.int32)
        self.offset = np.zeros((bands, rows, blocks), np.int32)
        self.unit_row = np.zeros((bands, ring, slots), np.int32)
        self.unit_pole = np.zeros((bands, ring, slots), np.int32)
        self.unit_on = np.zeros((bands, ring, slots), np.int32)
        self.unit_offset = np.zeros((bands, ring, slots), np.int32)
        self.height = 8
        for b in range(bands):
            ids = np.arange(rows) + b * rows
            self.row_on[b] = polar[ids]
            self.row_pole[b] = np.where(polar[ids], poles[ids], 0)
            held = [[] for _ in range(ring)]
            load = [0] * ring
            units = [(ranks[poles[ids[i]]], i, c) for i in range(rows) if polar[ids[i]] for c in range(blocks)]
            for rank, i, c in sorted(units, key=lambda u: (-u[0], u[1], u[2])):
                d = min((e for e in range(ring) if len(held[e]) < slots), key=lambda e: (load[e], e))
                held[d].append((i, c, rank))
                load[d] += rank
            self.height = max(self.height, max(load))
            for d in range(ring):
                start = 0
                for n, (i, c, rank) in enumerate(sorted(held[d])):
                    self.dest[b, i, c], self.offset[b, i, c] = d, start
                    self.unit_row[b, d, n], self.unit_on[b, d, n] = i, 1
                    self.unit_pole[b, d, n], self.unit_offset[b, d, n] = poles[ids[i]], start
                    start += rank


def pack_kernel(plan, pole, on, dest, offset, x_ref, basis_ref, out_ref, hold):
    i = pl.program_id(0)
    width, blocks = plan.width, dest.shape[0] // on.shape[0]

    @pl.when(i == 0)
    def _():
        hold[...] = jnp.zeros_like(hold)

    @pl.when(on[i] != 0)
    def _():
        z = three(split_table(basis_ref[0]), x_ref[0], plan.sub_pad)
        for c in range(blocks):
            at = pl.multiple_of(offset[i * blocks + c], 8)
            hold[dest[i * blocks + c], pl.ds(at, plan.rank), :] = z[:, c * width : (c + 1) * width]

    @pl.when(i == pl.num_programs(0) - 1)
    def _():
        out_ref[...] = hold[:, : plan.height, :]


def unit_kernel(plan, sub, padded, pole, on, offset, w_ref, basis_ref, basis_t_ref, table_ref, twist_ref, gain_ref, out_ref, came, hold, x_row, y_row):
    i = pl.program_id(0)
    ring, width = w_ref.shape[0], plan.width
    segment = basis_ref.shape[1]

    @pl.when(i == 0)
    def _():
        hold[...] = jnp.zeros_like(hold)
        came[:, : plan.height, :] = w_ref[...]
        came[:, plan.height :, :] = jnp.zeros((ring, plan.rank, width), jnp.float32)

    @pl.when(on[i] != 0)
    def _():
        at = pl.multiple_of(offset[i], 8)
        z = jnp.concatenate([came[j, pl.ds(at, plan.rank), :] for j in range(ring)], axis=1)
        x = three(split_table(basis_ref[0]), z, plan.rank_pad)
        for j in range(ring):
            x_row[pl.ds(j * segment, segment), :] = x[:, j * width : (j + 1) * width]
        filter_row(sub, padded, x_row, table_ref, twist_ref, gain_ref[0], y_row)
        y = jnp.concatenate([y_row[pl.ds(j * segment, segment), :] for j in range(ring)], axis=1)
        z = three(split_table(basis_t_ref[0]), y, plan.sub_pad)
        for j in range(ring):
            hold[j, pl.ds(at, plan.rank), :] = z[:, j * width : (j + 1) * width]

    @pl.when(i == pl.num_programs(0) - 1)
    def _():
        out_ref[...] = hold[:, : plan.height, :]


def unpack_kernel(plan, pole, on, dest, offset, w_ref, x_ref, scale_ref, basis_ref, rest_ref, y_ref, came):
    i = pl.program_id(0)
    ring, width = w_ref.shape[0], plan.width
    blocks = dest.shape[0] // on.shape[0]

    @pl.when(i == 0)
    def _():
        came[:, : plan.height, :] = w_ref[...]
        came[:, plan.height :, :] = jnp.zeros((ring, plan.rank, width), jnp.float32)

    @pl.when(on[i] == 0)
    def _():
        y_ref[...] = x_ref[...]

    @pl.when(on[i] != 0)
    def _():
        parts = []
        for c in range(blocks):
            at = pl.multiple_of(offset[i * blocks + c], 8)
            parts.append(came[dest[i * blocks + c], pl.ds(at, plan.rank), :])
        coef = jnp.concatenate(parts, axis=1)
        low = three(split_table(basis_ref[0]), coef, plan.rank_pad)
        high = three(split_table(rest_ref[0]), x_ref[0], plan.sub_pad)
        y_ref[0] = low + high * scale_ref[i]


def local(ring, bands, fields, cutoff):
    rows, segment, channels = fields.shape
    length = ring * segment
    sub = length // RADIX
    padded = -(-sub // 128) * 128
    plan = Plan(rows, segment, channels, ring, bands)
    width, height, rank = plan.width, plan.height, plan.rank
    band, me = lax.axis_index("lat"), lax.axis_index("lon")
    params = pltpu.CompilerParams(vmem_limit_bytes=56 * 1024 * 1024)
    f32 = jnp.float32

    pick = lambda a, *at: functools.reduce(lambda t, n: lax.dynamic_index_in_dim(t, n, 0, False), at, jnp.asarray(a))
    pole, on = pick(plan.row_pole, band), pick(plan.row_on, band)
    dest, offset = pick(plan.dest, band).reshape(-1), pick(plan.offset, band).reshape(-1)
    unit_row, unit_on = pick(plan.unit_row, band, me), pick(plan.unit_on, band, me)
    unit_pole, unit_offset = pick(plan.unit_pole, band, me), pick(plan.unit_offset, band, me)
    cut = cutoff.astype(f32)
    scale = jnp.sin(cut * f32(math.pi / length)) ** 2 / jnp.asarray(plan.top)[pole]
    gains = jnp.stack([gain_table(cut[unit_row[n]], sub, length) for n in range(plan.slots)])

    by_row = pl.BlockSpec((1, segment, channels), lambda i, *s: (i, 0, 0))
    by_pole = lambda a: pl.BlockSpec((1,) + a.shape[1:], lambda i, pole, *s: (pole[i], 0, 0))
    whole = lambda a: pl.BlockSpec(a.shape, lambda i, *s: (0,) * a.ndim)
    sent = jax.ShapeDtypeStruct((ring, height, width), f32)
    buffer = pltpu.VMEM((ring, height + rank, width), f32)

    packed = pl.pallas_call(
        functools.partial(pack_kernel, plan),
        out_shape=sent,
        grid_spec=pltpu.PrefetchScalarGridSpec(
            num_scalar_prefetch=4,
            grid=(rows,),
            in_specs=[by_row, by_pole(plan.basis_t)],
            out_specs=whole(sent),
            scratch_shapes=[buffer],
        ),
        compiler_params=params,
        name="pack",
    )(pole, on, dest, offset, fields, plan.basis_t)
    packed = lax.all_to_all(packed, "lon", 0, 0, tiled=True)
    table = fourier_table(sub, padded)
    twist = twist_table(sub, length)
    packed = pl.pallas_call(
        functools.partial(unit_kernel, plan, sub, padded),
        out_shape=sent,
        grid_spec=pltpu.PrefetchScalarGridSpec(
            num_scalar_prefetch=3,
            grid=(plan.slots,),
            in_specs=[
                whole(sent),
                by_pole(plan.basis),
                by_pole(plan.basis_t),
                whole(table),
                whole(twist),
                pl.BlockSpec((1,) + gains.shape[1:], lambda i, *s: (i, 0, 0)),
            ],
            out_specs=whole(sent),
            scratch_shapes=[buffer, buffer, pltpu.VMEM((length, width), f32), pltpu.VMEM((length, width), f32)],
        ),
        compiler_params=params,
        name="unit_filter",
    )(unit_pole, unit_on, unit_offset, packed, plan.basis, plan.basis_t, table, twist, gains)
    packed = lax.all_to_all(packed, "lon", 0, 0, tiled=True)
    return pl.pallas_call(
        functools.partial(unpack_kernel, plan),
        out_shape=jax.ShapeDtypeStruct(fields.shape, fields.dtype),
        grid_spec=pltpu.PrefetchScalarGridSpec(
            num_scalar_prefetch=4,
            grid=(rows,),
            in_specs=[
                whole(sent),
                by_row,
                pl.BlockSpec(memory_space=pltpu.SMEM),
                by_pole(plan.basis),
                by_pole(plan.rest),
            ],
            out_specs=by_row,
            scratch_shapes=[buffer],
        ),
        compiler_params=params,
        name="unpack",
    )(pole, on, dest, offset, packed, fields, scale, plan.basis, plan.rest)


def solution(mesh):
    return jax.shard_map(
        functools.partial(local, mesh.shape["lon"], mesh.shape["lat"]),
        mesh=mesh,
        in_specs=(P("lat", "lon", None), P("lat")),
        out_specs=P("lat", "lon", None),
        check_vma=False,
    )
```

profile of v0, /device:TPU:0, one launch (start us, length us, event | category | flops | bytes accessed | tf_op | source)
XLA Modules:
  0.0 103.5 jit_solution(17195011946533482726)
XLA Ops:
  0.0 0.7 constant_dynamic-slice_fusion.4
  0.7 0.6 reshape.51.offset
  1.3 0.6 reshape.50.dest
  1.9 1.3 %fusion.6 = (s32[8]{0:T(128)}, s32[8]{0:T(128)}) fusion(s32[4,8]{1,0:T(4,128)} %constant.152.clone, s32[]{:T(128)S(6)} %select_n.52, s32[4,8]{1,0:T(4,128)} %constant.151.clone), kind=kLoop, calls=%fused_computation.21 | loop fusion | bytes 132 | tf_op jit(solution)/shard_map/jit(dynamic_index_in_dim)/squeeze | solution.py:290
  3.2 0.0 copy-start.6
  3.2 0.0 copy-start.3
  3.2 0.0 copy-start.4
  3.2 0.0 copy-start.5
  3.2 9.5 %pack.1 = f32[8,352,128]{2,1,0:T(8,128)} custom-call(s32[8]{0:T(128)} %get-tuple-element.17.pole, s32[8]{0:T(128)} %get-tuple-element.16.on, s32[24]{0:T(128)} %reshape.50.dest, s32[24]{0:T(128)} %reshape.51.offset, f32[8,360,384]{2,1,0:T(8,128)} %x_ref.3, f32[10,240,384]{2,1,0:T(8,128)} %constant.163.clone.basis_ref.basis_t_ref), custom_call_target="tpu_custom_call" | custom-call | tf_op jit(solution)/shard_map/pack/pallas_call | solution.py:305
  12.7 5.2 %all-to-all-start = ((f32[8,352,128]{2,1,0:T(8,128)}), f32[8,352,128]{2,1,0:T(8,128)S(1)}, u32[]{:S(2)}, u32[]{:S(2)}) async-start(f32[8,352,128]{2,1,0:T(8,128)} %pack.1), calls=%async_computation | async-start | bytes 2883584 | tf_op jit(solution)/shard_map/all_to_all | solution.py:318
  17.9 0.7 constant_dynamic-slice_fusion
  18.6 0.7 fusion.13
  23.0 0.0 copy-done.6
  24.9 0.7 fusion.12
  27.7 1.2 %fusion.9.offset = s32[3]{0:T(128)} fusion(s32[4,8,3]{2,1,0:T(8,128)} %constant.158.clone, s32[]{:T(128)S(6)} %select_n.53, s32[]{:T(128)S(6)} %select_n.55), kind=kLoop, calls=%fused_computation.24 | loop fusion | bytes 32 | tf_op jit(solution)/shard_map/jit(dynamic_index_in_dim)/squeeze | solution.py:290
  28.9 1.2 %fusion.7 = (s32[3]{0:T(128)}, s32[3]{0:T(128)}) fusion(s32[4,8,3]{2,1,0:T(8,128)} %constant.157.clone, s32[]{:T(128)S(6)} %select_n.53, s32[]{:T(128)S(6)} %select_n.55, s32[4,8,3]{2,1,0:T(8,128)} %constant.156.clone), kind=kLoop, calls=%fused_computation.22 | loop fusion | bytes 56 | tf_op jit(solution)/shard_map/jit(dynamic_index_in_dim)/squeeze | solution.py:290
  30.1 0.0 copy-done.3
  30.1 0.0 copy-done.4
  30.1 0.0 copy-done.5
  30.1 1.9 %fusion.5 = (f32[1,360,5]{2,1,0:T(8,128)S(1)}, f32[1,360,5]{2,1,0:T(8,128)S(1)}, f32[1,360,5]{2,1,0:T(8,128)S(1)}) fusion(f32[360,5]{1,0:T(8,128)S(1)} %copy-done.3, f32[360,5]{1,0:T(8,128)S(1)} %copy-done.4, f32[]{:T(128)S(6)} %multiply.9, f32[5]{0:T(128)S(1)} %copy-done.5, f32[]{:T(128)} %bitcast.6, f32[]{:T(128)S(6)} %multiply.11, f32[]{:T(128)} %bitcast.12, ...), kind=kLoop, calls=%fused_computation.10 | loop fusion | flops 21600 | bytes 36044 | tf_op jit(solution)/shard_map/stack | solution.py:297
  32.1 0.9 pad_maximum_fusion.gain_ref
  32.9 4.5 %all-to-all-done.w_ref = f32[8,352,128]{2,1,0:T(8,128)S(1)} async-done(((f32[8,352,128]{2,1,0:T(8,128)}), f32[8,352,128]{2,1,0:T(8,128)S(1)}, u32[]{:S(2)}, u32[]{:S(2)}) %all-to-all-start) | async-done | bytes 1441824 | tf_op jit(solution)/shard_map/all_to_all | solution.py:318
  37.5 0.0 copy-start.1
  37.5 1.1 %copy-done.1 = f32[8,352,128]{2,1,0:T(8,128)} copy-done((f32[8,352,128]{2,1,0:T(8,128)}, f32[8,352,128]{2,1,0:T(8,128)S(1)}, u32[]{:S(2)}) %copy-start.1) | copy-done | bytes 1441816
  38.6 0.0 copy-start
  38.6 27.2 %unit_filter.1 = f32[8,352,128]{2,1,0:T(8,128)} custom-call(s32[3]{0:T(128)} %get-tuple-element.18.pole, s32[3]{0:T(128)} %get-tuple-element.19.on, s32[3]{0:T(128)} %fusion.9.offset, f32[8,352,128]{2,1,0:T(8,128)} %copy-done.1, f32[10,360,256]{2,1,0:T(8,128)} %constant.164.clone.basis_ref, f32[10,240,384]{2,1,0:T(8,128)} %constant.163.clone.basis_ref.basis_t_ref, ...), custom_call_target="tpu_custom_call" | custom-call | tf_op jit(solution)/shard_map/unit_filter/pallas_call | solution.py:321
  65.8 3.6 %all-to-all-start.1 = ((f32[8,352,128]{2,1,0:T(8,128)}), f32[8,352,128]{2,1,0:T(8,128)S(1)}, u32[]{:S(2)}, u32[]{:S(2)}) async-start(f32[8,352,128]{2,1,0:T(8,128)} %unit_filter.1), calls=%async_computation.1 | async-start | bytes 2883584 | tf_op jit(solution)/shard_map/all_to_all | solution.py:341
  69.4 0.7 fusion.10
  70.1 0.0 copy-done
  70.1 0.6 gather_fusion
  70.7 0.6 multiply_divide_fusion.scale_ref
  71.4 17.5 %all-to-all-done.1.w_ref = f32[8,352,128]{2,1,0:T(8,128)S(1)} async-done(((f32[8,352,128]{2,1,0:T(8,128)}), f32[8,352,128]{2,1,0:T(8,128)S(1)}, u32[]{:S(2)}, u32[]{:S(2)}) %all-to-all-start.1) | async-done | bytes 1441824 | tf_op jit(solution)/shard_map/all_to_all | solution.py:341
  88.9 0.0 copy-start.2
  88.9 1.1 %copy-done.2 = f32[8,352,128]{2,1,0:T(8,128)} copy-done((f32[8,352,128]{2,1,0:T(8,128)}, f32[8,352,128]{2,1,0:T(8,128)S(1)}, u32[]{:S(2)}) %copy-start.2) | copy-done | bytes 1441816
  90.0 13.5 %unpack.1 = f32[8,360,384]{2,1,0:T(8,128)} custom-call(s32[8]{0:T(128)} %get-tuple-element.17.pole, s32[8]{0:T(128)} %get-tuple-element.16.on, s32[24]{0:T(128)} %reshape.50.dest, s32[24]{0:T(128)} %reshape.51.offset, f32[8,352,128]{2,1,0:T(8,128)} %copy-done.2, f32[8,360,384]{2,1,0:T(8,128)} %x_ref.3, f32[8]{0:T(128)} %multiply_divide_fusion.scale_ref, ...), custom_call_target="tpu_custom_call" | custom-call | tf_op jit(solution)/shard_map/unpack/pallas_call | solution.py:342
  (2 shorter events, 0.0 us)
Async XLA Ops:
  3.2 19.8 %copy-start.6 = (s32[8]{0:T(128)S(1)}, s32[8]{0:T(128)}, u32[]{:S(2)}) copy-start(s32[8]{0:T(128)} %param.26) | copy-start | bytes 100
  3.2 27.0 %copy-start.3 = (f32[360,5]{1,0:T(8,128)S(1)}, f32[360,5]{1,0:T(8,128)}, u32[]{:S(2)}) copy-start(f32[360,5]{1,0:T(8,128)} %constant.168) | copy-start | bytes 21604
  3.2 27.0 %copy-start.4 = (f32[360,5]{1,0:T(8,128)S(1)}, f32[360,5]{1,0:T(8,128)}, u32[]{:S(2)}) copy-start(f32[360,5]{1,0:T(8,128)} %constant.161.clone) | copy-start | bytes 21604
  3.2 27.0 %copy-start.5 = (f32[5]{0:T(128)S(1)}, f32[5]{0:T(128)}, u32[]{:S(2)}) copy-start(f32[5]{0:T(128)} %constant.169) | copy-start | bytes 64
  12.7 24.8 %all-to-all-start = ((f32[8,352,128]{2,1,0:T(8,128)}), f32[8,352,128]{2,1,0:T(8,128)S(1)}, u32[]{:S(2)}, u32[]{:S(2)}) async-start(f32[8,352,128]{2,1,0:T(8,128)} %pack.1), calls=%async_computation | async-start | bytes 2883584 | tf_op jit(solution)/shard_map/all_to_all | solution.py:318
  37.5 1.1 %copy-start.1 = (f32[8,352,128]{2,1,0:T(8,128)}, f32[8,352,128]{2,1,0:T(8,128)S(1)}, u32[]{:S(2)}) copy-start(f32[8,352,128]{2,1,0:T(8,128)S(1)} %all-to-all-done.w_ref) | copy-start | bytes 4325380
  38.6 31.5 %copy-start = (f32[10]{0:T(128)S(1)}, f32[10]{0:T(128)}, u32[]{:S(2)}) copy-start(f32[10]{0:T(128)} %constant.159.clone) | copy-start | bytes 124
  65.8 23.1 %all-to-all-start.1 = ((f32[8,352,128]{2,1,0:T(8,128)}), f32[8,352,128]{2,1,0:T(8,128)S(1)}, u32[]{:S(2)}, u32[]{:S(2)}) async-start(f32[8,352,128]{2,1,0:T(8,128)} %unit_filter.1), calls=%async_computation.1 | async-start | bytes 2883584 | tf_op jit(solution)/shard_map/all_to_all | solution.py:341
  88.9 1.1 %copy-start.2 = (f32[8,352,128]{2,1,0:T(8,128)}, f32[8,352,128]{2,1,0:T(8,128)S(1)}, u32[]{:S(2)}) copy-start(f32[8,352,128]{2,1,0:T(8,128)S(1)} %all-to-all-done.1.w_ref) | copy-start | bytes 4325380
where the time goes:
time: 104 us
  Pallas kernels  50.2 us (48%)
  waiting for transfers between devices  22.1 us (21%)
  local copies, waits for them, and re-layouts  10.5 us (10%)
  starting transfers between devices  8.77 us (8%)
  between operations  7.77 us (7%)
  other arithmetic  4.13 us (4%)
    pallas_call x1, Pallas kernels, local(): pl.pallas_call(functools.partial(unit_kernel, plan, sub, padded), out_sha...  27.2 us
    all_to_all x2, waiting for transfers between devices, local(): packed = lax.all_to_all(packed, 'lon', 0, 0, tiled=True)  22.1 us
    pallas_call x1, Pallas kernels, local(): pl.pallas_call(functools.partial(unpack_kernel, plan), out_shape=jax.Shap...  13.5 us
    pallas_call x1, Pallas kernels, local(): pl.pallas_call(functools.partial(pack_kernel, plan), out_shape=sent, grid...  9.52 us
    all_to_all x2, starting transfers between devices, local(): packed = lax.all_to_all(packed, 'lon', 0, 0, tiled=True)  8.77 us
    squeeze x3, local copies, waits for them, and re-layouts, local(): lax.dynamic_index_in_dim(t, n, 0, False)  3.75 us
    another operation x2, other arithmetic, local(): jnp.stack([gain_table(cut[unit_row[n]], sub, length) for n in range(plan....  2.8 us
    unnamed x14, local copies, waits for them, and re-layouts  2.22 us
  transfers between devices with their start and end apart: 2, of which 2 were waited for; matrix products, arithmetic and copies ran while one was open for 9% of the time, Pallas kernels for 0%

commit v1 on v0

v1 whole, which is shorter than its diff:
```python
import functools

import jax
import jax.numpy as jnp
import numpy as np
from jax import lax
from jax.experimental import pallas as pl
from jax.experimental.pallas import tpu as pltpu
from jax.sharding import PartitionSpec as P

LANES = 128
SHAPES = 15
SLOT = 2 * SHAPES + 2
PER_TILE = LANES // SLOT
NEAR_RANK, FAR_RANK = 12, 4
MESH = pl.DeviceIdType.MESH


def filter_lines(cuts, length):
    wave = np.arange(length)
    folded = np.minimum(wave, length - wave)
    sine = np.sin(np.pi * np.maximum(folded, 1) / length)
    cuts = np.asarray(cuts)[:, None]
    gain = np.where(folded[None] <= cuts, 1.0, (np.sin(np.pi * cuts / length) / sine[None]) ** 2)
    return np.fft.ifft(gain, axis=1).real


def hankel(line, segment, distance):
    first = segment * distance - (segment - 1)
    wrapped = np.take(line, np.arange(first, first + 2 * segment - 1), mode="wrap")
    return np.lib.stride_tricks.sliding_window_view(wrapped, segment)


def envelope_shapes(length, segment, top):
    spot = np.arange(segment)
    family = [(a / (spot + a)) ** p for a in np.geomspace(0.3, 2 * segment, 40) for p in (1, 2, 3)]
    unit = 2.0 * spot / (segment - 1) - 1.0
    family += [np.polynomial.chebyshev.chebval(unit, [0] * j + [1]) for j in range(8)]
    left, size, _ = np.linalg.svd(np.array(family).T, full_matrices=False)
    left = left[:, size > 1e-6 * size[0]]
    cuts = np.unique(np.round(np.geomspace(1, top, 40)).astype(int))
    parts = []
    for cut, line in zip(cuts, filter_lines(cuts, length)):
        turn = 2.0 * np.pi * cut / length * spot[:, None]
        both = np.concatenate([left * np.cos(turn), left * np.sin(turn)], axis=1)
        u, s, vt = np.linalg.svd(both, full_matrices=False)
        keep = s > 1e-5 * s[0]
        inverse = (vt[keep].T / s[keep]) @ u[:, keep].T
        for distance in range(1, min(length // segment // 2, 4) + 1):
            u, s, _ = np.linalg.svd(inverse @ hankel(line, segment, distance), full_matrices=False)
            scaled = (u * s)[:, s > 1e-7]
            parts += [scaled[: left.shape[1]], scaled[left.shape[1] :]]
    u, _, _ = np.linalg.svd(np.concatenate(parts, axis=1), full_matrices=False)
    shapes = left @ u[:, :SHAPES]
    return np.pad(shapes, ((0, 0), (0, SHAPES - shapes.shape[1])))


@functools.lru_cache(maxsize=None)
def filter_tables(length, segment, top):
    shapes = envelope_shapes(length, segment, top)
    spot = np.arange(segment)
    cuts = np.arange(1, top + 1)
    lines = filter_lines(cuts, length)
    half = length // segment // 2
    ranks = [NEAR_RANK] + [FAR_RANK] * (half - 1)
    mixing = np.zeros((-(-(top + 1) // PER_TILE), sum(ranks), LANES))
    for cut, line in zip(cuts, lines):
        turn = 2.0 * np.pi * ((cut * spot) % length)[:, None] / length
        both = np.concatenate([shapes * np.cos(turn), shapes * np.sin(turn)], axis=1)
        u, s, vt = np.linalg.svd(both, full_matrices=False)
        keep = s > 3e-4 * s[0]
        u, back = u[:, keep], vt[keep].T / s[keep]
        at, start = (cut % PER_TILE) * SLOT, 0
        for distance, rank in enumerate(ranks, 1):
            inner = u.T @ (hankel(line, segment, distance) @ u)
            size, vectors = np.linalg.eigh((inner + inner.T) / 2.0)
            order = np.argsort(-np.abs(size), kind="stable")[:rank]
            count = len(order)
            weights = (back @ vectors[:, order]).T
            here = mixing[cut // PER_TILE, start : start + count, at : at + SLOT]
            here[:, :SHAPES] = weights[:, :SHAPES]
            here[:, SHAPES + 1 : 2 * SHAPES + 1] = weights[:, SHAPES:]
            here[:, SHAPES] = size[order]
            start += rank
    padded = -(-segment // LANES) * LANES
    away = np.abs(np.arange(2 * padded) - (padded - 1))
    mirrored = np.concatenate([np.zeros((1, 2 * padded)), lines[:, away]], axis=0)
    bank = np.zeros((2, SHAPES + 1, padded))
    bank[0, :SHAPES, :segment] = shapes.T
    bank[1, :SHAPES, :segment] = shapes[::-1].T
    return mirrored.astype(np.float32), mixing.astype(np.float32), bank.astype(np.float32), ranks


def split(a):
    hi = a.astype(jnp.bfloat16)
    lo = (a - hi.astype(jnp.float32)).astype(jnp.bfloat16)
    return hi, lo


def polar_row(band, bands, rows, i):
    total = rows * bands
    return jnp.abs(2 * (band * rows + i) + 1 - total) * 5 > 2 * total


class Layout:
    def __init__(self, rows, segment, channels, ring, ranks):
        self.rows, self.segment, self.channels, self.ring = rows, segment, channels, ring
        self.padded = -(-segment // LANES) * LANES
        self.half = ring // 2
        self.ranks = ranks
        self.count = sum(ranks)
        starts = np.concatenate([[0], np.cumsum(ranks)]).astype(int)
        plus = [(d, self.count + starts[d - 1], starts[d - 1], ranks[d - 1]) for d in range(1, self.half + 1)]
        minus = [(ring - d, starts[d - 1], self.count + starts[d - 1], ranks[d - 1]) for d in range(1, self.half)]
        self.peers, at = [], 0
        for step, send_row, come_row, rank in plus + minus:
            self.peers.append((step, int(send_row), int(come_row), rank, at))
            at += rank * rows
        self.total = at


def exchange_kernel(lay, bands, x_hbm, cut_ref, line_ref, mix_ref, bank_ref, y_hbm, come_ref, m_ref, x_buf, y_buf, send, xs, x_sem, y_sem, send_sem, recv_sem):
    seg, pad, ring, pairs = lay.segment, lay.padded, lay.ring, lay.rows // 2
    band, me = lax.axis_index("lat"), lax.axis_index("lon")
    barrier = pltpu.get_barrier_semaphore()
    length = seg * ring

    def fetch(p):
        return pltpu.make_async_copy(x_hbm.at[pl.ds(2 * p, 2)], x_buf.at[pl.ds(2 * p, 2)], x_sem.at[p])

    def store(p):
        return pltpu.make_async_copy(y_buf.at[pl.ds(2 * p, 2)], y_hbm.at[pl.ds(2 * p, 2)], y_sem.at[p])

    def push(n, p):
        step, _, _, rank, at = lay.peers[n]
        rows = pl.ds(pl.multiple_of(at + 2 * rank * p, 8), 2 * rank)
        return pltpu.make_async_remote_copy(
            src_ref=send.at[rows],
            dst_ref=come_ref.at[rows],
            send_sem=send_sem.at[n, p],
            recv_sem=recv_sem.at[n, p],
            device_id={"lon": lax.rem(me + step, ring)},
            device_id_type=MESH,
        )

    for p in range(pairs):
        fetch(p).start()
    for step in range(1, ring):
        pl.semaphore_signal(barrier, inc=1, device_id={"lon": lax.rem(me + step, ring)}, device_id_type=MESH)
    xs[...] = jnp.zeros_like(xs)
    pl.semaphore_wait(barrier, ring - 1)

    spot = lax.broadcasted_iota(jnp.int32, (1, pad), 1).astype(jnp.float32)
    slot = lax.broadcasted_iota(jnp.int32, (lay.count, LANES), 1)

    def basis(cut, flip):
        turn = cut * ((seg - 1.0) - spot if flip else spot)
        turn = turn - jnp.floor(turn * (1.0 / length)) * length
        angle = turn * (2.0 * np.pi / length)
        shapes = bank_ref[int(flip)]
        both = jnp.concatenate([shapes * jnp.cos(angle), shapes * jnp.sin(angle)], axis=0)
        return jnp.concatenate([both] * PER_TILE, axis=0)

    def one(i):
        x = x_buf[i]
        hi, lo = split(x)
        xs[0:seg] = hi
        xs[pad : pad + seg] = hi
        xs[2 * pad : 2 * pad + seg] = lo
        cut = cut_ref[i]
        which = lax.rem(cut, PER_TILE)
        mix = jnp.where(slot // SLOT == which, mix_ref[i], 0.0)
        size = jnp.sum(jnp.where(lax.rem(slot, SLOT) == SHAPES, mix, 0.0), axis=1, keepdims=True)
        cut = cut.astype(jnp.float32)
        dot = functools.partial(jnp.dot, precision=lax.Precision.HIGHEST, preferred_element_type=jnp.float32)
        m = jnp.concatenate([dot(mix, basis(cut, False)), dot(mix, basis(cut, True)) * size], axis=0)
        m_ref[i] = m
        hi, lo = split(m)
        wide = xs[...]
        a = jnp.dot(jnp.concatenate([hi, lo, hi], axis=1), wide, preferred_element_type=jnp.float32)
        line = jnp.broadcast_to(line_ref[pl.ds(i, 1), :], (LANES, 2 * pad))
        sheet = pltpu.roll(line, 2 * pad - (LANES - 1), 1, stride=1, stride_axis=0)[:, : 2 * pad - LANES]
        hi, lo = split(sheet)
        on = polar_row(band, bands, lay.rows, i)
        for q in range(pad // LANES):
            cols = slice(pad - LANES * (q + 1), 2 * pad - LANES * (q + 1))
            left = jnp.concatenate([hi[:, cols], lo[:, cols], hi[:, cols]], axis=1)
            rows = min(LANES, seg - q * LANES)
            y = jnp.dot(left, wide, preferred_element_type=jnp.float32)[:rows]
            block = slice(q * LANES, q * LANES + rows)
            y_buf[i, block, :] = jnp.where(on, y, x[block])
        return a

    @pl.loop(0, pairs)
    def _(p):
        fetch(p).wait()
        first, second = one(2 * p), one(2 * p + 1)
        for n, (_, row, _, rank, at) in enumerate(lay.peers):
            both = jnp.concatenate([first[row : row + rank], second[row : row + rank]], axis=0)
            send[pl.ds(pl.multiple_of(at + 2 * rank * p, 8), 2 * rank), :] = both
        for n in range(ring - 1):
            push(n, p).start()
        store(p).start()

    @pl.loop(0, pairs)
    def _(p):
        store(p).wait()
        for n in range(ring - 1):
            push(n, p).wait()


def join_kernel(lay, bands, y_ref, come_ref, m_ref, out_ref):
    p = pl.program_id(0)
    band = lax.axis_index("lat")
    for r in range(2):
        parts = [None] * (2 * lay.count)
        for _, _, row, rank, at in lay.peers:
            both = come_ref[pl.ds(pl.multiple_of(at + 2 * rank * p, 8), 2 * rank), :]
            parts[row] = both[r * rank : (r + 1) * rank]
        gap = 2 * lay.count - sum(v.shape[0] for v in parts if v is not None)
        last = lay.count + sum(lay.ranks[:-1])
        parts[last] = jnp.zeros((gap, lay.channels), jnp.float32)
        b = jnp.concatenate([v for v in parts if v is not None], axis=0)
        m_hi, m_lo = split(m_ref[r])
        b_hi, b_lo = split(b)
        left = jnp.concatenate([m_hi, m_lo, m_hi], axis=0)
        right = jnp.concatenate([b_hi, b_hi, b_lo], axis=0)
        far = lax.dot_general(left, right, (((0,), (0,)), ((), ())), preferred_element_type=jnp.float32)
        y = y_ref[r]
        out_ref[r] = jnp.where(polar_row(band, bands, lay.rows, 2 * p + r), y + far[: lay.segment], y)


def local(ring, bands, fields, cutoff):
    rows, segment, channels = fields.shape
    length, total = ring * segment, rows * bands
    row_ids = np.arange(total)
    polar = np.abs(2 * row_ids + 1 - total) * 5 > 2 * total
    poles = np.minimum(row_ids, total - 1 - row_ids)
    top = int(1 + (length // 2 - 1) * (2 * poles[polar].max() + 1) // total)
    lines, mixing, bank, ranks = filter_tables(length, segment, top)
    lay = Layout(rows, segment, channels, ring, ranks)
    pad = lay.padded
    cut = jnp.clip(cutoff, 1, top)
    line = jnp.asarray(lines)[cut]
    mix = jnp.asarray(mixing)[cut // PER_TILE]
    f32 = jnp.float32
    any_space = pl.BlockSpec(memory_space=pl.ANY)
    vmem = pl.BlockSpec(memory_space=pltpu.VMEM)
    partial, come, m = pl.pallas_call(
        functools.partial(exchange_kernel, lay, bands),
        out_shape=[
            jax.ShapeDtypeStruct(fields.shape, f32),
            jax.ShapeDtypeStruct((lay.total, channels), f32),
            jax.ShapeDtypeStruct((rows, 2 * lay.count, pad), f32),
        ],
        in_specs=[any_space, pl.BlockSpec(memory_space=pltpu.SMEM), vmem, vmem, vmem],
        out_specs=[any_space, vmem, vmem],
        scratch_shapes=[
            pltpu.VMEM(fields.shape, f32),
            pltpu.VMEM(fields.shape, f32),
            pltpu.VMEM((lay.total, channels), f32),
            pltpu.VMEM((3 * pad, channels), jnp.bfloat16),
            pltpu.SemaphoreType.DMA((rows // 2,)),
            pltpu.SemaphoreType.DMA((rows // 2,)),
            pltpu.SemaphoreType.DMA((ring - 1, rows // 2)),
            pltpu.SemaphoreType.DMA((ring - 1, rows // 2)),
        ],
        compiler_params=pltpu.CompilerParams(collective_id=0, has_side_effects=True, vmem_limit_bytes=40 * 1024 * 1024),
        name="exchange",
    )(fields, cut, line, mix, bank)
    by_pair = lambda a: pl.BlockSpec((2,) + a.shape[1:], lambda p: (p, 0, 0))
    return pl.pallas_call(
        functools.partial(join_kernel, lay, bands),
        out_shape=jax.ShapeDtypeStruct(fields.shape, fields.dtype),
        grid=(rows // 2,),
        in_specs=[by_pair(partial), pl.BlockSpec(come.shape, lambda p: (0, 0)), by_pair(m)],
        out_specs=by_pair(fields),
        compiler_params=pltpu.CompilerParams(vmem_limit_bytes=40 * 1024 * 1024),
        name="join",
    )(partial, come, m)


def solution(mesh):
    return jax.shard_map(
        functools.partial(local, mesh.shape["lon"], mesh.shape["lat"]),
        mesh=mesh,
        in_specs=(P("lat", "lon", None), P("lat")),
        out_specs=P("lat", "lon", None),
        check_vma=False,
    )
```

time: 104 us -> 29.6 us (0.28)
  Pallas kernels: 50.2 us -> 21 us
  waiting for transfers between devices: 22.1 us -> 0 us
  starting transfers between devices: 8.77 us -> 0 us
  between operations: 7.77 us -> 0.04 us
  other arithmetic: 4.13 us -> 0.67 us
  local copies, waits for them, and re-layouts: 10.5 us -> 7.66 us
    pallas_call x3 -> x2, Pallas kernels: 50.2 us -> 21 us  [the longest x1 17.7 us: local(): pl.pallas_call(functools.partial(exchange_kernel, lay, bands), out_shape=...]
    all_to_all x2 -> x0, waiting for transfers between devices: 22.1 us -> none  [local(): packed = lax.all_to_all(packed, 'lon', 0, 0, tiled=True)]
    all_to_all x2 -> x0, starting transfers between devices: 8.77 us -> none  [local(): packed = lax.all_to_all(packed, 'lon', 0, 0, tiled=True)]
    gather x1 -> x2, local copies, waits for them, and re-layouts: 0.64 us -> 4.62 us  [the longest x1 2.32 us: local(): line = jnp.asarray(lines)[cut]]
    squeeze x3 -> x0, local copies, waits for them, and re-layouts: 3.75 us -> none  [local(): lax.dynamic_index_in_dim(t, n, 0, False)]
    another operation x2 -> x0, other arithmetic: 2.8 us -> none  [local(): jnp.stack([gain_table(cut[unit_row[n]], sub, length) for n in range(plan....]
    dynamic_slice x3 -> x0, local copies, waits for them, and re-layouts: 2.07 us -> none  [the longest x2 1.4 us: local(): lax.dynamic_index_in_dim(t, n, 0, False)]
    reshape x2 -> x0, local copies, waits for them, and re-layouts: 1.18 us -> none  [the longest x1 0.62 us: local(): pick(plan.offset, band).reshape(-1)]
  transfers between devices with their start and end apart: 2 -> 0, of which waited for: 2 -> 0; matrix products, arithmetic and copies ran while one was open for 9% -> 0% of each run, Pallas kernels for 0% -> 0%
where the time goes in v1:
time: 29.6 us; the launch traced here: 29.4 us
  Pallas kernels  21 us (71%)
  local copies, waits for them, and re-layouts  7.66 us (26%)
  other arithmetic  0.67 us (2%)
    pallas_call x1, Pallas kernels, local(): pl.pallas_call(functools.partial(exchange_kernel, lay, bands), out_shape=...  17.7 us
    pallas_call x1, Pallas kernels, local(): pl.pallas_call(functools.partial(join_kernel, lay, bands), out_shape=jax....  3.26 us
    unnamed x4, local copies, waits for them, and re-layouts  3.05 us
    gather x1, local copies, waits for them, and re-layouts, local(): line = jnp.asarray(lines)[cut]  2.32 us
    gather x1, local copies, waits for them, and re-layouts, local(): mix = jnp.asarray(mixing)[cut // PER_TILE]  2.3 us
    select_n x1, other arithmetic, local(): mix = jnp.asarray(mixing)[cut // PER_TILE]  0.67 us

profile of v1, /device:TPU:0, one launch (start us, length us, event | category | flops | bytes accessed | tf_op | source)
XLA Modules:
  0.0 29.4 jit_solution(15590618660475182482)
XLA Ops:
  0.0 0.7 %compare_select_fusion = (s32[8]{0:T(128)S(1)}, s32[8]{0:T(128)S(1)}, s32[8]{0:T(128)S(1)}) fusion(s32[8]{0:T(128)} %param.6), kind=kLoop, calls=%fused_computation.4 | loop fusion | flops 168 | bytes 128 | tf_op jit(solution)/shard_map/select_n | solution.py:245
  0.7 2.3 %gather_fusion = f32[8,768]{1,0:T(8,128)S(1)} fusion(f32[856,768]{1,0:T(8,128)} %constant.30.clone, s32[1024]{0:T(1024)S(1)} %get-tuple-element.15), kind=kCustom, calls=%fused_computation | custom fusion | bytes 49184 | tf_op jit(solution)/shard_map/gather | solution.py:244
  3.0 2.3 %gather_fusion.1 = f32[8,24,128]{2,1,0:T(8,128)S(1)} fusion(f32[214,24,128]{2,1,0:T(8,128)} %constant.31.clone, s32[1024]{0:T(1024)S(1)} %get-tuple-element.14), kind=kCustom, calls=%fused_computation.1 | custom fusion | bytes 196640 | tf_op jit(solution)/shard_map/gather | solution.py:245
  5.3 0.0 copy-start
  5.3 2.2 %copy-done = f32[8,360,384]{2,1,0:T(8,128)S(1)} copy-done((f32[8,360,384]{2,1,0:T(8,128)S(1)}, f32[8,360,384]{2,1,0:T(8,128)}, u32[]{:S(2)}) %copy-start) | copy-done | bytes 4423704
  7.6 0.0 copy-start.1
  7.6 0.8 %copy-done.1 = f32[2,16,384]{2,1,0:T(8,128)S(1)} copy-done((f32[2,16,384]{2,1,0:T(8,128)S(1)}, f32[2,16,384]{2,1,0:T(8,128)}, u32[]{:S(2)}) %copy-start.1) | copy-done | bytes 49176
  8.4 17.7 %exchange.1 = (f32[8,360,384]{2,1,0:T(8,128)S(1)}, f32[352,384]{1,0:T(8,128)S(1)}, f32[8,48,384]{2,1,0:T(8,128)S(1)}) custom-call(f32[8,360,384]{2,1,0:T(8,128)S(1)} %copy-done, s32[8]{0:T(128)S(1)} %get-tuple-element.13.cut_ref, f32[8,768]{1,0:T(8,128)S(1)} %gather_fusion, f32[8,24,128]{2,1,0:T(8,128)S(1)} %gather_fusion.1, f32[2,16,384]{2,1,0:T(8,128)S(1)} %copy-done.1), custom_call_target="tpu_custom_call" | custom-call | tf_op jit(solution)/shard_map/exchange/pallas_call | solution.py:249
  26.1 3.3 %join.1 = f32[8,360,384]{2,1,0:T(8,128)} custom-call(f32[8,360,384]{2,1,0:T(8,128)S(1)} %get-tuple-element.8.y_ref, f32[352,384]{1,0:T(8,128)S(1)} %get-tuple-element.9.come_ref, f32[8,48,384]{2,1,0:T(8,128)S(1)} %get-tuple-element.10.m_ref), custom_call_target="tpu_custom_call" | custom-call | tf_op jit(solution)/shard_map/join/pallas_call | solution.py:272
  (1 shorter events, 0.0 us)
Async XLA Ops:
  5.3 2.3 %copy-start = (f32[8,360,384]{2,1,0:T(8,128)S(1)}, f32[8,360,384]{2,1,0:T(8,128)}, u32[]{:S(2)}) copy-start(f32[8,360,384]{2,1,0:T(8,128)} %x_hbm.1) | copy-start | bytes 13271044
  7.6 0.8 %copy-start.1 = (f32[2,16,384]{2,1,0:T(8,128)S(1)}, f32[2,16,384]{2,1,0:T(8,128)}, u32[]{:S(2)}) copy-start(f32[2,16,384]{2,1,0:T(8,128)} %constant.32.clone.bank_ref) | copy-start | bytes 147460

commit v2 on v1

--- a/solution.py
+++ b/solution.py
@@ -84,11 +84,18 @@
             start += rank
     padded = -(-segment // LANES) * LANES
     away = np.abs(np.arange(2 * padded) - (padded - 1))
-    mirrored = np.concatenate([np.zeros((1, 2 * padded)), lines[:, away]], axis=0)
-    bank = np.zeros((2, SHAPES + 1, padded))
-    bank[0, :SHAPES, :segment] = shapes.T
-    bank[1, :SHAPES, :segment] = shapes[::-1].T
-    return mirrored.astype(np.float32), mixing.astype(np.float32), bank.astype(np.float32), ranks
+    tiles = -(-2 * padded // LANES // 8) * 8
+    mirrored = np.zeros((mixing.shape[0] * PER_TILE, tiles * LANES))
+    mirrored[1 : top + 1, : 2 * padded] = lines[:, away]
+    table = np.concatenate([mirrored.reshape(-1, PER_TILE * tiles, LANES), mixing], axis=1)
+    tail = np.zeros((2,) + table.shape[1:])
+    for flip in range(2):
+        bank = np.zeros((SHAPES + 1, padded))
+        bank[:SHAPES, :segment] = (shapes[::-1] if flip else shapes).T
+        for k in range(padded // LANES):
+            tail[flip, k * (SHAPES + 1) : (k + 1) * (SHAPES + 1)] = bank[:, k * LANES : (k + 1) * LANES]
+    table = np.concatenate([table, tail], axis=0)
+    return table.astype(np.float32), tiles, ranks
 
 
 def split(a):
@@ -107,6 +114,7 @@
         self.rows, self.segment, self.channels, self.ring = rows, segment, channels, ring
         self.padded = -(-segment // LANES) * LANES
         self.half = ring // 2
+        self.tall = -(-(2 * sum(ranks) + segment) // 16) * 16
         self.ranks = ranks
         self.count = sum(ranks)
         starts = np.concatenate([[0], np.cumsum(ranks)]).astype(int)
@@ -119,17 +127,64 @@
         self.total = at
 
 
-def exchange_kernel(lay, bands, x_hbm, cut_ref, line_ref, mix_ref, bank_ref, y_hbm, come_ref, m_ref, x_buf, y_buf, send, xs, x_sem, y_sem, send_sem, recv_sem):
+def three(a):
+    hi = a.astype(jnp.bfloat16)
+    rest = a - hi.astype(jnp.float32)
+    mid = rest.astype(jnp.bfloat16)
+    return hi, mid, (rest - mid.astype(jnp.float32)).astype(jnp.bfloat16)
+
+
+def lookup_kernel(lay, top, cut_ref, table_hbm, line_ref, left_ref, bank_buf, mix_buf, bank_sem, line_sem, mix_sem):
+    rows, seg, pad, length = lay.rows, lay.segment, lay.padded, lay.segment * lay.ring
+    tiles = line_ref.shape[1]
+    cuts = [jnp.clip(cut_ref[i], 1, top) for i in range(rows)]
+    lines, mixes = [], []
+    shapes = pltpu.make_async_copy(table_hbm.at[pl.ds(table_hbm.shape[0] - 2, 2), pl.ds(0, bank_buf.shape[1])], bank_buf, bank_sem)
+    shapes.start()
+    for i in range(rows):
+        group = table_hbm.at[cuts[i] // PER_TILE]
+        start = pl.multiple_of(lax.rem(cuts[i], PER_TILE) * tiles, 8)
+        mixes.append(pltpu.make_async_copy(group.at[pl.ds(PER_TILE * tiles, lay.count)], mix_buf.at[i], mix_sem.at[i]))
+        lines.append(pltpu.make_async_copy(group.at[pl.ds(start, tiles)], line_ref.at[i], line_sem.at[i]))
+    for copy in mixes + lines:
+        copy.start()
+
+    row = lax.broadcasted_iota(jnp.int32, (rows, pad), 0)
+    spot = lax.broadcasted_iota(jnp.int32, (rows, pad), 1).astype(jnp.float32)
+    cut = functools.reduce(lambda v, i: jnp.where(row == i, cuts[i].astype(jnp.float32), v), range(rows), jnp.zeros((rows, pad), jnp.float32))
+
+    def waves(turn):
+        turn = turn - jnp.floor(turn * (1.0 / length)) * length
+        angle = turn * (2.0 * np.pi / length)
+        return jnp.cos(angle), jnp.sin(angle)
+
+    ahead, behind = waves(cut * spot), waves(cut * ((seg - 1.0) - spot))
+    slot = lax.broadcasted_iota(jnp.int32, (lay.count, LANES), 1)
+    shapes.wait()
+    step = SHAPES + 1
+    bank = [jnp.concatenate([bank_buf[f, k * step : (k + 1) * step] for k in range(pad // LANES)], axis=1) for f in range(2)]
+    for i in range(rows):
+        basis = [jnp.concatenate([bank[f] * w[i : i + 1] for w in pair], axis=0) for f, pair in enumerate((ahead, behind))]
+        hi, mid, lo = three(jnp.concatenate(basis, axis=1))
+        right = jnp.concatenate([hi, mid, lo, hi, mid, hi], axis=0)
+        mixes[i].wait()
+        mix = jnp.where(slot // SLOT == lax.rem(cuts[i], PER_TILE), mix_buf[i], 0.0)
+        size = jnp.sum(jnp.where(lax.rem(slot, SLOT) == SHAPES, mix, 0.0), axis=1, keepdims=True)
+        mix = functools.reduce(jnp.add, [mix[:, k * SLOT : (k + 1) * SLOT] for k in range(PER_TILE)])
+        hi, mid, lo = three(mix)
+        left = jnp.concatenate([hi, hi, hi, mid, mid, lo], axis=1)
+        q = jnp.dot(left, right, preferred_element_type=jnp.float32)
+        hi, lo = split(jnp.concatenate([q[:, :pad], q[:, pad:] * size], axis=0))
+        left_ref[i] = jnp.concatenate([hi, lo, hi], axis=1)
+    for copy in lines:
+        copy.wait()
+
+
+def exchange_kernel(lay, bands, x_ref, line_ref, left_ref, y_ref, come_ref, send, xs, left, send_sem, recv_sem):
     seg, pad, ring, pairs = lay.segment, lay.padded, lay.ring, lay.rows // 2
+    tops = 2 * lay.count
     band, me = lax.axis_index("lat"), lax.axis_index("lon")
     barrier = pltpu.get_barrier_semaphore()
-    length = seg * ring
-
-    def fetch(p):
-        return pltpu.make_async_copy(x_hbm.at[pl.ds(2 * p, 2)], x_buf.at[pl.ds(2 * p, 2)], x_sem.at[p])
-
-    def store(p):
-        return pltpu.make_async_copy(y_buf.at[pl.ds(2 * p, 2)], y_hbm.at[pl.ds(2 * p, 2)], y_sem.at[p])
 
     def push(n, p):
         step, _, _, rank, at = lay.peers[n]
@@ -143,68 +198,48 @@
             device_id_type=MESH,
         )
 
-    for p in range(pairs):
-        fetch(p).start()
     for step in range(1, ring):
         pl.semaphore_signal(barrier, inc=1, device_id={"lon": lax.rem(me + step, ring)}, device_id_type=MESH)
     xs[...] = jnp.zeros_like(xs)
-    pl.semaphore_wait(barrier, ring - 1)
-
-    spot = lax.broadcasted_iota(jnp.int32, (1, pad), 1).astype(jnp.float32)
-    slot = lax.broadcasted_iota(jnp.int32, (lay.count, LANES), 1)
-
-    def basis(cut, flip):
-        turn = cut * ((seg - 1.0) - spot if flip else spot)
-        turn = turn - jnp.floor(turn * (1.0 / length)) * length
-        angle = turn * (2.0 * np.pi / length)
-        shapes = bank_ref[int(flip)]
-        both = jnp.concatenate([shapes * jnp.cos(angle), shapes * jnp.sin(angle)], axis=0)
-        return jnp.concatenate([both] * PER_TILE, axis=0)
-
-    def one(i):
-        x = x_buf[i]
+
+    def one(i, s):
+        x = x_ref[i]
         hi, lo = split(x)
-        xs[0:seg] = hi
-        xs[pad : pad + seg] = hi
-        xs[2 * pad : 2 * pad + seg] = lo
-        cut = cut_ref[i]
-        which = lax.rem(cut, PER_TILE)
-        mix = jnp.where(slot // SLOT == which, mix_ref[i], 0.0)
-        size = jnp.sum(jnp.where(lax.rem(slot, SLOT) == SHAPES, mix, 0.0), axis=1, keepdims=True)
-        cut = cut.astype(jnp.float32)
-        dot = functools.partial(jnp.dot, precision=lax.Precision.HIGHEST, preferred_element_type=jnp.float32)
-        m = jnp.concatenate([dot(mix, basis(cut, False)), dot(mix, basis(cut, True)) * size], axis=0)
-        m_ref[i] = m
-        hi, lo = split(m)
-        wide = xs[...]
-        a = jnp.dot(jnp.concatenate([hi, lo, hi], axis=1), wide, preferred_element_type=jnp.float32)
-        line = jnp.broadcast_to(line_ref[pl.ds(i, 1), :], (LANES, 2 * pad))
+        xs[s, 0:seg] = hi
+        xs[s, pad : pad + seg] = hi
+        xs[s, 2 * pad : 2 * pad + seg] = lo
+        left[s, 0:tops] = left_ref[i]
+        line = line_ref[i]
+        line = jnp.concatenate([jnp.broadcast_to(line[k : k + 1], (LANES, LANES)) for k in range(2 * pad // LANES)], axis=1)
         sheet = pltpu.roll(line, 2 * pad - (LANES - 1), 1, stride=1, stride_axis=0)[:, : 2 * pad - LANES]
         hi, lo = split(sheet)
-        on = polar_row(band, bands, lay.rows, i)
         for q in range(pad // LANES):
             cols = slice(pad - LANES * (q + 1), 2 * pad - LANES * (q + 1))
-            left = jnp.concatenate([hi[:, cols], lo[:, cols], hi[:, cols]], axis=1)
-            rows = min(LANES, seg - q * LANES)
-            y = jnp.dot(left, wide, preferred_element_type=jnp.float32)[:rows]
-            block = slice(q * LANES, q * LANES + rows)
-            y_buf[i, block, :] = jnp.where(on, y, x[block])
-        return a
+            rows = min(LANES, lay.tall - tops - q * LANES)
+            block = slice(tops + q * LANES, tops + q * LANES + rows)
+            left[s, block, 0:pad] = hi[:rows, cols]
+            left[s, block, pad : 2 * pad] = lo[:rows, cols]
+            left[s, block, 2 * pad : 3 * pad] = hi[:rows, cols]
+        both = jnp.dot(left[s], xs[s], preferred_element_type=jnp.float32)
+        y_ref[i] = jnp.where(polar_row(band, bands, lay.rows, i), both[tops : tops + seg], x)
+        return both[:tops]
 
     @pl.loop(0, pairs)
     def _(p):
-        fetch(p).wait()
-        first, second = one(2 * p), one(2 * p + 1)
-        for n, (_, row, _, rank, at) in enumerate(lay.peers):
+        first, second = one(2 * p, 0), one(2 * p + 1, 1)
+        for _, row, _, rank, at in lay.peers:
             both = jnp.concatenate([first[row : row + rank], second[row : row + rank]], axis=0)
             send[pl.ds(pl.multiple_of(at + 2 * rank * p, 8), 2 * rank), :] = both
+
+        @pl.when(p == 0)
+        def _():
+            pl.semaphore_wait(barrier, ring - 1)
+
         for n in range(ring - 1):
             push(n, p).start()
-        store(p).start()
 
     @pl.loop(0, pairs)
     def _(p):
-        store(p).wait()
         for n in range(ring - 1):
             push(n, p).wait()
 
@@ -221,9 +256,9 @@
         last = lay.count + sum(lay.ranks[:-1])
         parts[last] = jnp.zeros((gap, lay.channels), jnp.float32)
         b = jnp.concatenate([v for v in parts if v is not None], axis=0)
-        m_hi, m_lo = split(m_ref[r])
+        pad = lay.padded
         b_hi, b_lo = split(b)
-        left = jnp.concatenate([m_hi, m_lo, m_hi], axis=0)
+        left = jnp.concatenate([m_ref[r, :, k * pad : (k + 1) * pad] for k in range(3)], axis=0)
         right = jnp.concatenate([b_hi, b_hi, b_lo], axis=0)
         far = lax.dot_general(left, right, (((0,), (0,)), ((), ())), preferred_element_type=jnp.float32)
         y = y_ref[r]
@@ -237,47 +272,59 @@
     polar = np.abs(2 * row_ids + 1 - total) * 5 > 2 * total
     poles = np.minimum(row_ids, total - 1 - row_ids)
     top = int(1 + (length // 2 - 1) * (2 * poles[polar].max() + 1) // total)
-    lines, mixing, bank, ranks = filter_tables(length, segment, top)
+    table, tiles, ranks = filter_tables(length, segment, top)
     lay = Layout(rows, segment, channels, ring, ranks)
     pad = lay.padded
-    cut = jnp.clip(cutoff, 1, top)
-    line = jnp.asarray(lines)[cut]
-    mix = jnp.asarray(mixing)[cut // PER_TILE]
     f32 = jnp.float32
-    any_space = pl.BlockSpec(memory_space=pl.ANY)
+    hbm = pl.BlockSpec(memory_space=pltpu.HBM)
     vmem = pl.BlockSpec(memory_space=pltpu.VMEM)
-    partial, come, m = pl.pallas_call(
+    params = functools.partial(pltpu.CompilerParams, vmem_limit_bytes=24 * 1024 * 1024)
+    line, left = pl.pallas_call(
+        functools.partial(lookup_kernel, lay, top),
+        out_shape=[
+            jax.ShapeDtypeStruct((rows, tiles, LANES), f32),
+            jax.ShapeDtypeStruct((rows, 2 * lay.count, 3 * pad), jnp.bfloat16),
+        ],
+        in_specs=[pl.BlockSpec(memory_space=pltpu.SMEM), hbm],
+        out_specs=[vmem, vmem],
+        scratch_shapes=[
+            pltpu.VMEM((2, (SHAPES + 1) * pad // LANES, LANES), f32),
+            pltpu.VMEM((rows, lay.count, LANES), f32),
+            pltpu.SemaphoreType.DMA,
+            pltpu.SemaphoreType.DMA((rows,)),
+            pltpu.SemaphoreType.DMA((rows,)),
+        ],
+        compiler_params=pltpu.CompilerParams(vmem_limit_bytes=52 * 1024 * 1024),
+        name="lookup",
+    )(cutoff, table)
+    partial, come = pl.pallas_call(
         functools.partial(exchange_kernel, lay, bands),
         out_shape=[
             jax.ShapeDtypeStruct(fields.shape, f32),
             jax.ShapeDtypeStruct((lay.total, channels), f32),
-            jax.ShapeDtypeStruct((rows, 2 * lay.count, pad), f32),
         ],
-        in_specs=[any_space, pl.BlockSpec(memory_space=pltpu.SMEM), vmem, vmem, vmem],
-        out_specs=[any_space, vmem, vmem],
+        in_specs=[vmem, vmem, vmem],
+        out_specs=[vmem, vmem],
         scratch_shapes=[
-            pltpu.VMEM(fields.shape, f32),
-            pltpu.VMEM(fields.shape, f32),
             pltpu.VMEM((lay.total, channels), f32),
-            pltpu.VMEM((3 * pad, channels), jnp.bfloat16),
-            pltpu.SemaphoreType.DMA((rows // 2,)),
-            pltpu.SemaphoreType.DMA((rows // 2,)),
+            pltpu.VMEM((2, 3 * pad, channels), jnp.bfloat16),
+            pltpu.VMEM((2, lay.tall, 3 * pad), jnp.bfloat16),
             pltpu.SemaphoreType.DMA((ring - 1, rows // 2)),
             pltpu.SemaphoreType.DMA((ring - 1, rows // 2)),
         ],
-        compiler_params=pltpu.CompilerParams(collective_id=0, has_side_effects=True, vmem_limit_bytes=40 * 1024 * 1024),
+        compiler_params=params(collective_id=0, has_side_effects=True),
         name="exchange",
-    )(fields, cut, line, mix, bank)
+    )(fields, line, left)
     by_pair = lambda a: pl.BlockSpec((2,) + a.shape[1:], lambda p: (p, 0, 0))
     return pl.pallas_call(
         functools.partial(join_kernel, lay, bands),
         out_shape=jax.ShapeDtypeStruct(fields.shape, fields.dtype),
         grid=(rows // 2,),
-        in_specs=[by_pair(partial), pl.BlockSpec(come.shape, lambda p: (0, 0)), by_pair(m)],
+        in_specs=[by_pair(partial), pl.BlockSpec(come.shape, lambda p: (0, 0)), by_pair(left)],
         out_specs=by_pair(fields),
-        compiler_params=pltpu.CompilerParams(vmem_limit_bytes=40 * 1024 * 1024),
+        compiler_params=params(),
         name="join",
-    )(partial, come, m)
+    )(partial, come, left)
 
 
 def solution(mesh):

time: 29.6 us -> 20.8 us (0.70)
  local copies, waits for them, and re-layouts: 7.66 us -> 0.66 us
  Pallas kernels: 21 us -> 20 us
  other arithmetic: 0.67 us -> 0 us
    pallas_call x1, Pallas kernels: 17.7 us -> 12.3 us  [local(): pl.pallas_call(functools.partial(exchange_kernel, lay, bands), out_shape=...]
    gather x2 -> x0, local copies, waits for them, and re-layouts: 4.62 us -> none  [the longest x1 2.32 us: local(): line = jnp.asarray(lines)[cut]]
    pallas_call x0 -> x1, Pallas kernels: none -> 4.44 us  [local(): pl.pallas_call(functools.partial(lookup_kernel, lay, top), out_shape=[jax...]
    unnamed x4, local copies, waits for them, and re-layouts: 3.05 us -> 0.66 us
    select_n x1 -> x0, other arithmetic: 0.67 us -> none  [local(): mix = jnp.asarray(mixing)[cut // PER_TILE]]
where the time goes in v2:
time: 20.8 us; the launch traced here: 20.7 us
  Pallas kernels  20 us (96%)
  local copies, waits for them, and re-layouts  0.66 us (3%)
    pallas_call x1, Pallas kernels, local(): pl.pallas_call(functools.partial(exchange_kernel, lay, bands), out_shape=...  12.3 us
    pallas_call x1, Pallas kernels, local(): pl.pallas_call(functools.partial(lookup_kernel, lay, top), out_shape=[jax...  4.44 us
    pallas_call x1, Pallas kernels, local(): pl.pallas_call(functools.partial(join_kernel, lay, bands), out_shape=jax....  3.25 us
    unnamed x4, local copies, waits for them, and re-layouts  0.66 us

profile of v2, /device:TPU:0, one launch (start us, length us, event | category | flops | bytes accessed | tf_op | source)
XLA Modules:
  0.0 20.7 jit_solution(3748741823745726086)
XLA Ops:
  0.0 0.0 copy-start.1
  0.0 0.7 %copy-done.1 = s32[8]{0:T(128)S(1)} copy-done((s32[8]{0:T(128)S(1)}, s32[8]{0:T(128)}, u32[]{:S(2)}) %copy-start.1) | copy-done | bytes 56
  0.7 0.0 copy-start
  0.7 4.4 %lookup.1 = (f32[8,8,128]{2,1,0:T(8,128)S(1)}, bf16[8,48,1152]{2,1,0:T(8,128)(2,1)S(1)}) custom-call(s32[8]{0:T(128)S(1)} %copy-done.1, f32[216,56,128]{2,1,0:T(8,128)} %constant.2.clone.table_hbm), custom_call_target="tpu_custom_call" | custom-call | tf_op jit(solution)/shard_map/lookup/pallas_call | solution.py:282
  5.1 0.0 copy-done
  5.1 12.3 %exchange.1 = (f32[8,360,384]{2,1,0:T(8,128)S(1)}, f32[352,384]{1,0:T(8,128)S(1)}) custom-call(f32[8,360,384]{2,1,0:T(8,128)S(1)} %copy-done, f32[8,8,128]{2,1,0:T(8,128)S(1)} %get-tuple-element.9.line_ref, bf16[8,48,1152]{2,1,0:T(8,128)(2,1)S(1)} %get-tuple-element.10.left_ref.m_ref), custom_call_target="tpu_custom_call" | custom-call | tf_op jit(solution)/shard_map/exchange/pallas_call | solution.py:300
  17.4 3.3 %join.1 = f32[8,360,384]{2,1,0:T(8,128)} custom-call(f32[8,360,384]{2,1,0:T(8,128)S(1)} %get-tuple-element.11.y_ref, f32[352,384]{1,0:T(8,128)S(1)} %get-tuple-element.12.come_ref, bf16[8,48,1152]{2,1,0:T(8,128)(2,1)S(1)} %get-tuple-element.10.left_ref.m_ref), custom_call_target="tpu_custom_call" | custom-call | tf_op jit(solution)/shard_map/join/pallas_call | solution.py:319
Async XLA Ops:
  0.0 0.7 %copy-start.1 = (s32[8]{0:T(128)S(1)}, s32[8]{0:T(128)}, u32[]{:S(2)}) copy-start(s32[8]{0:T(128)} %cut_ref.1) | copy-start | bytes 100
  0.7 4.5 %copy-start = (f32[8,360,384]{2,1,0:T(8,128)S(1)}, f32[8,360,384]{2,1,0:T(8,128)}, u32[]{:S(2)}) copy-start(f32[8,360,384]{2,1,0:T(8,128)} %x_ref.1) | copy-start | bytes 13271044

commit v3 on v2

--- a/solution.py
+++ b/solution.py
@@ -114,7 +114,7 @@
         self.rows, self.segment, self.channels, self.ring = rows, segment, channels, ring
         self.padded = -(-segment // LANES) * LANES
         self.half = ring // 2
-        self.tall = -(-(2 * sum(ranks) + segment) // 16) * 16
+        self.tall = -(-segment // 16) * 16
         self.ranks = ranks
         self.count = sum(ranks)
         starts = np.concatenate([[0], np.cumsum(ranks)]).astype(int)
@@ -134,55 +134,24 @@
     return hi, mid, (rest - mid.astype(jnp.float32)).astype(jnp.bfloat16)
 
 
-def lookup_kernel(lay, top, cut_ref, table_hbm, line_ref, left_ref, bank_buf, mix_buf, bank_sem, line_sem, mix_sem):
-    rows, seg, pad, length = lay.rows, lay.segment, lay.padded, lay.segment * lay.ring
-    tiles = line_ref.shape[1]
-    cuts = [jnp.clip(cut_ref[i], 1, top) for i in range(rows)]
-    lines, mixes = [], []
-    shapes = pltpu.make_async_copy(table_hbm.at[pl.ds(table_hbm.shape[0] - 2, 2), pl.ds(0, bank_buf.shape[1])], bank_buf, bank_sem)
-    shapes.start()
+def lookup_kernel(lay, top, cut_ref, table_hbm, line_ref, mix_ref, bank_ref, bank_sem, line_sem, mix_sem):
+    rows, tiles = lay.rows, line_ref.shape[1]
+    copies = [pltpu.make_async_copy(table_hbm.at[pl.ds(table_hbm.shape[0] - 2, 2), pl.ds(0, bank_ref.shape[1])], bank_ref, bank_sem)]
     for i in range(rows):
-        group = table_hbm.at[cuts[i] // PER_TILE]
-        start = pl.multiple_of(lax.rem(cuts[i], PER_TILE) * tiles, 8)
-        mixes.append(pltpu.make_async_copy(group.at[pl.ds(PER_TILE * tiles, lay.count)], mix_buf.at[i], mix_sem.at[i]))
-        lines.append(pltpu.make_async_copy(group.at[pl.ds(start, tiles)], line_ref.at[i], line_sem.at[i]))
-    for copy in mixes + lines:
+        cut = jnp.clip(cut_ref[i], 1, top)
+        group = table_hbm.at[cut // PER_TILE]
+        start = pl.multiple_of(lax.rem(cut, PER_TILE) * tiles, 8)
+        copies.append(pltpu.make_async_copy(group.at[pl.ds(PER_TILE * tiles, lay.count)], mix_ref.at[i], mix_sem.at[i]))
+        copies.append(pltpu.make_async_copy(group.at[pl.ds(start, tiles)], line_ref.at[i], line_sem.at[i]))
+    for copy in copies:
         copy.start()
-
-    row = lax.broadcasted_iota(jnp.int32, (rows, pad), 0)
-    spot = lax.broadcasted_iota(jnp.int32, (rows, pad), 1).astype(jnp.float32)
-    cut = functools.reduce(lambda v, i: jnp.where(row == i, cuts[i].astype(jnp.float32), v), range(rows), jnp.zeros((rows, pad), jnp.float32))
-
-    def waves(turn):
-        turn = turn - jnp.floor(turn * (1.0 / length)) * length
-        angle = turn * (2.0 * np.pi / length)
-        return jnp.cos(angle), jnp.sin(angle)
-
-    ahead, behind = waves(cut * spot), waves(cut * ((seg - 1.0) - spot))
-    slot = lax.broadcasted_iota(jnp.int32, (lay.count, LANES), 1)
-    shapes.wait()
-    step = SHAPES + 1
-    bank = [jnp.concatenate([bank_buf[f, k * step : (k + 1) * step] for k in range(pad // LANES)], axis=1) for f in range(2)]
-    for i in range(rows):
-        basis = [jnp.concatenate([bank[f] * w[i : i + 1] for w in pair], axis=0) for f, pair in enumerate((ahead, behind))]
-        hi, mid, lo = three(jnp.concatenate(basis, axis=1))
-        right = jnp.concatenate([hi, mid, lo, hi, mid, hi], axis=0)
-        mixes[i].wait()
-        mix = jnp.where(slot // SLOT == lax.rem(cuts[i], PER_TILE), mix_buf[i], 0.0)
-        size = jnp.sum(jnp.where(lax.rem(slot, SLOT) == SHAPES, mix, 0.0), axis=1, keepdims=True)
-        mix = functools.reduce(jnp.add, [mix[:, k * SLOT : (k + 1) * SLOT] for k in range(PER_TILE)])
-        hi, mid, lo = three(mix)
-        left = jnp.concatenate([hi, hi, hi, mid, mid, lo], axis=1)
-        q = jnp.dot(left, right, preferred_element_type=jnp.float32)
-        hi, lo = split(jnp.concatenate([q[:, :pad], q[:, pad:] * size], axis=0))
-        left_ref[i] = jnp.concatenate([hi, lo, hi], axis=1)
-    for copy in lines:
+    for copy in copies:
         copy.wait()
 
 
-def exchange_kernel(lay, bands, x_ref, line_ref, left_ref, y_ref, come_ref, send, xs, left, send_sem, recv_sem):
+def exchange_kernel(lay, bands, top, cut_ref, x_ref, line_ref, mix_ref, bank_ref, y_ref, come_ref, m_ref, send, xs, left, turns, send_sem, recv_sem):
     seg, pad, ring, pairs = lay.segment, lay.padded, lay.ring, lay.rows // 2
-    tops = 2 * lay.count
+    length = seg * ring
     band, me = lax.axis_index("lat"), lax.axis_index("lon")
     barrier = pltpu.get_barrier_semaphore()
 
@@ -200,35 +169,67 @@
 
     for step in range(1, ring):
         pl.semaphore_signal(barrier, inc=1, device_id={"lon": lax.rem(me + step, ring)}, device_id_type=MESH)
-    xs[...] = jnp.zeros_like(xs)
-
-    def one(i, s):
+
+    if pad != seg:
+        for r in range(lay.rows):
+            for k in range(3):
+                xs[r, k * pad + seg : (k + 1) * pad] = jnp.zeros((pad - seg, lay.channels), jnp.bfloat16)
+    row = lax.broadcasted_iota(jnp.int32, (lay.rows, pad), 0)
+    spot = lax.broadcasted_iota(jnp.int32, (lay.rows, pad), 1).astype(jnp.float32)
+    cut = jnp.zeros((lay.rows, pad), jnp.float32)
+    for i in range(lay.rows):
+        cut = jnp.where(row == i, jnp.clip(cut_ref[i], 1, top).astype(jnp.float32), cut)
+    for f, place in enumerate((spot, (seg - 1.0) - spot)):
+        turn = cut * place
+        turn = turn - jnp.floor(turn * (1.0 / length)) * length
+        angle = turn * (2.0 * np.pi / length)
+        turns[2 * f] = jnp.cos(angle)
+        turns[2 * f + 1] = jnp.sin(angle)
+    slot = lax.broadcasted_iota(jnp.int32, (lay.count, LANES), 1)
+    step = SHAPES + 1
+
+    def project(i):
         x = x_ref[i]
         hi, lo = split(x)
-        xs[s, 0:seg] = hi
-        xs[s, pad : pad + seg] = hi
-        xs[s, 2 * pad : 2 * pad + seg] = lo
-        left[s, 0:tops] = left_ref[i]
+        xs[i, 0:seg] = hi
+        xs[i, pad : pad + seg] = hi
+        xs[i, 2 * pad : 2 * pad + seg] = lo
+        basis = []
+        for f in range(2):
+            bank = jnp.concatenate([bank_ref[f, k * step : (k + 1) * step] for k in range(pad // LANES)], axis=1)
+            basis.append(jnp.concatenate([bank * turns[2 * f + w, pl.ds(i, 1), :] for w in range(2)], axis=0))
+        hi, mid, lo = three(jnp.concatenate(basis, axis=1))
+        right = jnp.concatenate([hi, mid, lo, hi, mid, hi], axis=0)
+        mix = jnp.where(slot // SLOT == lax.rem(jnp.clip(cut_ref[i], 1, top), PER_TILE), mix_ref[i], 0.0)
+        size = jnp.sum(jnp.where(lax.rem(slot, SLOT) == SHAPES, mix, 0.0), axis=1, keepdims=True)
+        mix = functools.reduce(jnp.add, [mix[:, k * SLOT : (k + 1) * SLOT] for k in range(PER_TILE)])
+        hi, mid, lo = three(mix)
+        q = jnp.dot(jnp.concatenate([hi, hi, hi, mid, mid, lo], axis=1), right, preferred_element_type=jnp.float32)
+        hi, lo = split(jnp.concatenate([q[:, :pad], q[:, pad:] * size], axis=0))
+        m = jnp.concatenate([hi, lo, hi], axis=1)
+        m_ref[i] = m
+        return jnp.dot(m, xs[i], preferred_element_type=jnp.float32)
+
+    def diagonal(i, s):
         line = line_ref[i]
         line = jnp.concatenate([jnp.broadcast_to(line[k : k + 1], (LANES, LANES)) for k in range(2 * pad // LANES)], axis=1)
         sheet = pltpu.roll(line, 2 * pad - (LANES - 1), 1, stride=1, stride_axis=0)[:, : 2 * pad - LANES]
         hi, lo = split(sheet)
         for q in range(pad // LANES):
             cols = slice(pad - LANES * (q + 1), 2 * pad - LANES * (q + 1))
-            rows = min(LANES, lay.tall - tops - q * LANES)
-            block = slice(tops + q * LANES, tops + q * LANES + rows)
+            rows = min(LANES, lay.tall - q * LANES)
+            block = slice(q * LANES, q * LANES + rows)
             left[s, block, 0:pad] = hi[:rows, cols]
             left[s, block, pad : 2 * pad] = lo[:rows, cols]
             left[s, block, 2 * pad : 3 * pad] = hi[:rows, cols]
-        both = jnp.dot(left[s], xs[s], preferred_element_type=jnp.float32)
-        y_ref[i] = jnp.where(polar_row(band, bands, lay.rows, i), both[tops : tops + seg], x)
-        return both[:tops]
+        y = jnp.dot(left[s], xs[i], preferred_element_type=jnp.float32)[:seg]
+        y_ref[i] = jnp.where(polar_row(band, bands, lay.rows, i), y, x_ref[i])
 
     @pl.loop(0, pairs)
     def _(p):
-        first, second = one(2 * p, 0), one(2 * p + 1, 1)
-        for _, row, _, rank, at in lay.peers:
-            both = jnp.concatenate([first[row : row + rank], second[row : row + rank]], axis=0)
+        first, second = project(2 * p), project(2 * p + 1)
+        for _, at_row, _, rank, at in lay.peers:
+            both = jnp.concatenate([first[at_row : at_row + rank], second[at_row : at_row + rank]], axis=0)
             send[pl.ds(pl.multiple_of(at + 2 * rank * p, 8), 2 * rank), :] = both
 
         @pl.when(p == 0)
@@ -237,6 +238,11 @@
 
         for n in range(ring - 1):
             push(n, p).start()
+
+    @pl.loop(0, pairs)
+    def _(p):
+        diagonal(2 * p, 0)
+        diagonal(2 * p + 1, 1)
 
     @pl.loop(0, pairs)
     def _(p):
@@ -279,17 +285,16 @@
     hbm = pl.BlockSpec(memory_space=pltpu.HBM)
     vmem = pl.BlockSpec(memory_space=pltpu.VMEM)
     params = functools.partial(pltpu.CompilerParams, vmem_limit_bytes=24 * 1024 * 1024)
-    line, left = pl.pallas_call(
+    line, mix, bank = pl.pallas_call(
         functools.partial(lookup_kernel, lay, top),
         out_shape=[
             jax.ShapeDtypeStruct((rows, tiles, LANES), f32),
-            jax.ShapeDtypeStruct((rows, 2 * lay.count, 3 * pad), jnp.bfloat16),
+            jax.ShapeDtypeStruct((rows, lay.count, LANES), f32),
+            jax.ShapeDtypeStruct((2, (SHAPES + 1) * pad // LANES, LANES), f32),
         ],
         in_specs=[pl.BlockSpec(memory_space=pltpu.SMEM), hbm],
-        out_specs=[vmem, vmem],
+        out_specs=[vmem] * 3,
         scratch_shapes=[
-            pltpu.VMEM((2, (SHAPES + 1) * pad // LANES, LANES), f32),
-            pltpu.VMEM((rows, lay.count, LANES), f32),
             pltpu.SemaphoreType.DMA,
             pltpu.SemaphoreType.DMA((rows,)),
             pltpu.SemaphoreType.DMA((rows,)),
@@ -297,24 +302,26 @@
         compiler_params=pltpu.CompilerParams(vmem_limit_bytes=52 * 1024 * 1024),
         name="lookup",
     )(cutoff, table)
-    partial, come = pl.pallas_call(
-        functools.partial(exchange_kernel, lay, bands),
+    partial, come, left = pl.pallas_call(
+        functools.partial(exchange_kernel, lay, bands, top),
         out_shape=[
             jax.ShapeDtypeStruct(fields.shape, f32),
             jax.ShapeDtypeStruct((lay.total, channels), f32),
+            jax.ShapeDtypeStruct((rows, 2 * lay.count, 3 * pad), jnp.bfloat16),
         ],
-        in_specs=[vmem, vmem, vmem],
-        out_specs=[vmem, vmem],
+        in_specs=[pl.BlockSpec(memory_space=pltpu.SMEM), vmem, vmem, vmem, vmem],
+        out_specs=[vmem] * 3,
         scratch_shapes=[
             pltpu.VMEM((lay.total, channels), f32),
-            pltpu.VMEM((2, 3 * pad, channels), jnp.bfloat16),
+            pltpu.VMEM((rows, 3 * pad, channels), jnp.bfloat16),
             pltpu.VMEM((2, lay.tall, 3 * pad), jnp.bfloat16),
+            pltpu.VMEM((4, rows, pad), f32),
             pltpu.SemaphoreType.DMA((ring - 1, rows // 2)),
             pltpu.SemaphoreType.DMA((ring - 1, rows // 2)),
         ],
         compiler_params=params(collective_id=0, has_side_effects=True),
         name="exchange",
-    )(fields, line, left)
+    )(cutoff, fields, line, mix, bank)
     by_pair = lambda a: pl.BlockSpec((2,) + a.shape[1:], lambda p: (p, 0, 0))
     return pl.pallas_call(
         functools.partial(join_kernel, lay, bands),

time: 20.8 us -> 19.3 us (0.928)
  Pallas kernels: 20 us -> 18 us
  local copies, waits for them, and re-layouts: 0.66 us -> 1.14 us
    pallas_call x1, Pallas kernels: 4.44 us -> 1.93 us  [local(): pl.pallas_call(functools.partial(lookup_kernel, lay, top), out_shape=[jax...]
    pallas_call x1, Pallas kernels: 12.3 us -> 12.9 us  [local(): pl.pallas_call(functools.partial(exchange_kernel, lay, bands, top), out_s...]
    unnamed x4, local copies, waits for them, and re-layouts: 0.66 us -> 1.14 us
where the time goes in v3:
time: 19.3 us; the launch traced here: 19.2 us
  Pallas kernels  18 us (93%)
  local copies, waits for them, and re-layouts  1.14 us (6%)
    pallas_call x1, Pallas kernels, local(): pl.pallas_call(functools.partial(exchange_kernel, lay, bands, top), out_s...  12.9 us
    pallas_call x1, Pallas kernels, local(): pl.pallas_call(functools.partial(join_kernel, lay, bands), out_shape=jax....  3.25 us
    pallas_call x1, Pallas kernels, local(): pl.pallas_call(functools.partial(lookup_kernel, lay, top), out_shape=[jax...  1.93 us
    unnamed x4, local copies, waits for them, and re-layouts  1.14 us

profile of v3, /device:TPU:0, one launch (start us, length us, event | category | flops | bytes accessed | tf_op | source)
XLA Modules:
  0.0 19.2 jit_solution(14580759239225688396)
XLA Ops:
  0.0 0.0 copy-start.1
  0.0 0.7 %copy-done.1 = s32[8]{0:T(128)S(1)} copy-done((s32[8]{0:T(128)S(1)}, s32[8]{0:T(128)}, u32[]{:S(2)}) %copy-start.1) | copy-done | bytes 56
  0.7 0.0 copy-start
  0.7 1.9 %lookup.1 = (f32[8,8,128]{2,1,0:T(8,128)S(1)}, f32[8,24,128]{2,1,0:T(8,128)S(1)}, f32[2,48,128]{2,1,0:T(8,128)S(1)}) custom-call(s32[8]{0:T(128)S(1)} %copy-done.1, f32[216,56,128]{2,1,0:T(8,128)} %constant.2.clone.table_hbm), custom_call_target="tpu_custom_call" | custom-call | tf_op jit(solution)/shard_map/lookup/pallas_call | solution.py:288
  2.6 0.5 %copy-done = f32[8,360,384]{2,1,0:T(8,128)S(1)} copy-done((f32[8,360,384]{2,1,0:T(8,128)S(1)}, f32[8,360,384]{2,1,0:T(8,128)}, u32[]{:S(2)}) %copy-start) | copy-done | bytes 4423704
  3.1 12.9 %exchange.1 = (f32[8,360,384]{2,1,0:T(8,128)S(1)}, f32[352,384]{1,0:T(8,128)S(1)}, bf16[8,48,1152]{2,1,0:T(8,128)(2,1)S(1)}) custom-call(s32[8]{0:T(128)S(1)} %copy-done.1, f32[8,360,384]{2,1,0:T(8,128)S(1)} %copy-done, f32[8,8,128]{2,1,0:T(8,128)S(1)} %get-tuple-element.11.line_ref, f32[8,24,128]{2,1,0:T(8,128)S(1)} %get-tuple-element.12.mix_ref, ...), custom_call_target="tpu_custom_call" | custom-call | tf_op jit(solution)/shard_map/exchange/pallas_call | solution.py:305
  15.9 3.3 %join.1 = f32[8,360,384]{2,1,0:T(8,128)} custom-call(f32[8,360,384]{2,1,0:T(8,128)S(1)} %get-tuple-element.14.y_ref, f32[352,384]{1,0:T(8,128)S(1)} %get-tuple-element.15.come_ref, bf16[8,48,1152]{2,1,0:T(8,128)(2,1)S(1)} %get-tuple-element.16.m_ref), custom_call_target="tpu_custom_call" | custom-call | tf_op jit(solution)/shard_map/join/pallas_call | solution.py:326
Async XLA Ops:
  0.0 0.7 %copy-start.1 = (s32[8]{0:T(128)S(1)}, s32[8]{0:T(128)}, u32[]{:S(2)}) copy-start(s32[8]{0:T(128)} %cut_ref.3) | copy-start | bytes 100
  0.7 2.4 %copy-start = (f32[8,360,384]{2,1,0:T(8,128)S(1)}, f32[8,360,384]{2,1,0:T(8,128)}, u32[]{:S(2)}) copy-start(f32[8,360,384]{2,1,0:T(8,128)} %x_ref.1) | copy-start | bytes 13271044

commit v4 on v3

--- a/solution.py
+++ b/solution.py
@@ -87,15 +87,11 @@
     tiles = -(-2 * padded // LANES // 8) * 8
     mirrored = np.zeros((mixing.shape[0] * PER_TILE, tiles * LANES))
     mirrored[1 : top + 1, : 2 * padded] = lines[:, away]
-    table = np.concatenate([mirrored.reshape(-1, PER_TILE * tiles, LANES), mixing], axis=1)
-    tail = np.zeros((2,) + table.shape[1:])
-    for flip in range(2):
-        bank = np.zeros((SHAPES + 1, padded))
-        bank[:SHAPES, :segment] = (shapes[::-1] if flip else shapes).T
-        for k in range(padded // LANES):
-            tail[flip, k * (SHAPES + 1) : (k + 1) * (SHAPES + 1)] = bank[:, k * LANES : (k + 1) * LANES]
-    table = np.concatenate([table, tail], axis=0)
-    return table.astype(np.float32), tiles, ranks
+    mirrored = mirrored.reshape(-1, tiles, LANES)
+    banks = np.zeros((2, SHAPES + 1, padded))
+    banks[0, :SHAPES, :segment] = shapes.T
+    banks[1, :SHAPES, :segment] = shapes[::-1].T
+    return mirrored.astype(np.float32), mixing.astype(np.float32), banks.astype(np.float32), ranks
 
 
 def split(a):
@@ -134,22 +130,7 @@
     return hi, mid, (rest - mid.astype(jnp.float32)).astype(jnp.bfloat16)
 
 
-def lookup_kernel(lay, top, cut_ref, table_hbm, line_ref, mix_ref, bank_ref, bank_sem, line_sem, mix_sem):
-    rows, tiles = lay.rows, line_ref.shape[1]
-    copies = [pltpu.make_async_copy(table_hbm.at[pl.ds(table_hbm.shape[0] - 2, 2), pl.ds(0, bank_ref.shape[1])], bank_ref, bank_sem)]
-    for i in range(rows):
-        cut = jnp.clip(cut_ref[i], 1, top)
-        group = table_hbm.at[cut // PER_TILE]
-        start = pl.multiple_of(lax.rem(cut, PER_TILE) * tiles, 8)
-        copies.append(pltpu.make_async_copy(group.at[pl.ds(PER_TILE * tiles, lay.count)], mix_ref.at[i], mix_sem.at[i]))
-        copies.append(pltpu.make_async_copy(group.at[pl.ds(start, tiles)], line_ref.at[i], line_sem.at[i]))
-    for copy in copies:
-        copy.start()
-    for copy in copies:
-        copy.wait()
-
-
-def exchange_kernel(lay, bands, top, cut_ref, x_ref, line_ref, mix_ref, bank_ref, y_ref, come_ref, m_ref, send, xs, left, turns, send_sem, recv_sem):
+def filter_kernel(lay, bands, top, cut_hbm, x_hbm, line_hbm, mix_hbm, bank_hbm, y_ref, cut_ref, x_ref, line_ref, mix_ref, bank_ref, come_ref, m_ref, send, xs, left, turns, load_sem, x_sem, send_sem, recv_sem):
     seg, pad, ring, pairs = lay.segment, lay.padded, lay.ring, lay.rows // 2
     length = seg * ring
     band, me = lax.axis_index("lat"), lax.axis_index("lon")
@@ -167,6 +148,18 @@
             device_id_type=MESH,
         )
 
+    def fetch(p):
+        return pltpu.make_async_copy(x_hbm.at[pl.ds(2 * p, 2)], x_ref.at[pl.ds(2 * p, 2)], x_sem.at[p])
+
+    loads = [
+        pltpu.make_async_copy(a, b, load_sem.at[k])
+        for k, (a, b) in enumerate(((cut_hbm, cut_ref), (bank_hbm, bank_ref), (mix_hbm, mix_ref), (line_hbm, line_ref)))
+    ]
+    for copy in loads[:3]:
+        copy.start()
+    for p in range(pairs):
+        fetch(p).start()
+    loads[3].start()
     for step in range(1, ring):
         pl.semaphore_signal(barrier, inc=1, device_id={"lon": lax.rem(me + step, ring)}, device_id_type=MESH)
 
@@ -174,6 +167,7 @@
         for r in range(lay.rows):
             for k in range(3):
                 xs[r, k * pad + seg : (k + 1) * pad] = jnp.zeros((pad - seg, lay.channels), jnp.bfloat16)
+    loads[0].wait()
     row = lax.broadcasted_iota(jnp.int32, (lay.rows, pad), 0)
     spot = lax.broadcasted_iota(jnp.int32, (lay.rows, pad), 1).astype(jnp.float32)
     cut = jnp.zeros((lay.rows, pad), jnp.float32)
@@ -186,7 +180,8 @@
         turns[2 * f] = jnp.cos(angle)
         turns[2 * f + 1] = jnp.sin(angle)
     slot = lax.broadcasted_iota(jnp.int32, (lay.count, LANES), 1)
-    step = SHAPES + 1
+    loads[1].wait()
+    loads[2].wait()
 
     def project(i):
         x = x_ref[i]
@@ -196,11 +191,11 @@
         xs[i, 2 * pad : 2 * pad + seg] = lo
         basis = []
         for f in range(2):
-            bank = jnp.concatenate([bank_ref[f, k * step : (k + 1) * step] for k in range(pad // LANES)], axis=1)
-            basis.append(jnp.concatenate([bank * turns[2 * f + w, pl.ds(i, 1), :] for w in range(2)], axis=0))
+            basis.append(jnp.concatenate([bank_ref[f] * turns[2 * f + w, pl.ds(i, 1), :] for w in range(2)], axis=0))
         hi, mid, lo = three(jnp.concatenate(basis, axis=1))
         right = jnp.concatenate([hi, mid, lo, hi, mid, hi], axis=0)
-        mix = jnp.where(slot // SLOT == lax.rem(jnp.clip(cut_ref[i], 1, top), PER_TILE), mix_ref[i], 0.0)
+        cut = jnp.clip(cut_ref[i], 1, top)
+        mix = jnp.where(slot // SLOT == lax.rem(cut, PER_TILE), mix_ref[cut // PER_TILE], 0.0)
         size = jnp.sum(jnp.where(lax.rem(slot, SLOT) == SHAPES, mix, 0.0), axis=1, keepdims=True)
         mix = functools.reduce(jnp.add, [mix[:, k * SLOT : (k + 1) * SLOT] for k in range(PER_TILE)])
         hi, mid, lo = three(mix)
@@ -211,7 +206,7 @@
         return jnp.dot(m, xs[i], preferred_element_type=jnp.float32)
 
     def diagonal(i, s):
-        line = line_ref[i]
+        line = line_ref[jnp.clip(cut_ref[i], 1, top)]
         line = jnp.concatenate([jnp.broadcast_to(line[k : k + 1], (LANES, LANES)) for k in range(2 * pad // LANES)], axis=1)
         sheet = pltpu.roll(line, 2 * pad - (LANES - 1), 1, stride=1, stride_axis=0)[:, : 2 * pad - LANES]
         hi, lo = split(sheet)
@@ -223,10 +218,23 @@
             left[s, block, pad : 2 * pad] = lo[:rows, cols]
             left[s, block, 2 * pad : 3 * pad] = hi[:rows, cols]
         y = jnp.dot(left[s], xs[i], preferred_element_type=jnp.float32)[:seg]
-        y_ref[i] = jnp.where(polar_row(band, bands, lay.rows, i), y, x_ref[i])
+        y_ref[i] = y
+
+    def finish(i, r, come):
+        parts = [None] * (2 * lay.count)
+        for (_, _, at_row, rank, _), both in zip(lay.peers, come):
+            parts[at_row] = both[r * rank : (r + 1) * rank]
+        unused = lay.count + sum(lay.ranks[:-1])
+        parts[unused] = jnp.zeros((lay.ranks[-1], lay.channels), jnp.float32)
+        hi, lo = split(jnp.concatenate([v for v in parts if v is not None], axis=0))
+        right = jnp.concatenate([hi, hi, lo], axis=0)
+        wide = jnp.concatenate([m_ref[i, :, k * pad : (k + 1) * pad] for k in range(3)], axis=0)
+        far = lax.dot_general(wide, right, (((0,), (0,)), ((), ())), preferred_element_type=jnp.float32)[:seg]
+        y_ref[i] = jnp.where(polar_row(band, bands, lay.rows, i), y_ref[i] + far, x_ref[i])
 
     @pl.loop(0, pairs)
     def _(p):
+        fetch(p).wait()
         first, second = project(2 * p), project(2 * p + 1)
         for _, at_row, _, rank, at in lay.peers:
             both = jnp.concatenate([first[at_row : at_row + rank], second[at_row : at_row + rank]], axis=0)
@@ -239,6 +247,8 @@
         for n in range(ring - 1):
             push(n, p).start()
 
+    loads[3].wait()
+
     @pl.loop(0, pairs)
     def _(p):
         diagonal(2 * p, 0)
@@ -248,27 +258,9 @@
     def _(p):
         for n in range(ring - 1):
             push(n, p).wait()
-
-
-def join_kernel(lay, bands, y_ref, come_ref, m_ref, out_ref):
-    p = pl.program_id(0)
-    band = lax.axis_index("lat")
-    for r in range(2):
-        parts = [None] * (2 * lay.count)
-        for _, _, row, rank, at in lay.peers:
-            both = come_ref[pl.ds(pl.multiple_of(at + 2 * rank * p, 8), 2 * rank), :]
-            parts[row] = both[r * rank : (r + 1) * rank]
-        gap = 2 * lay.count - sum(v.shape[0] for v in parts if v is not None)
-        last = lay.count + sum(lay.ranks[:-1])
-        parts[last] = jnp.zeros((gap, lay.channels), jnp.float32)
-        b = jnp.concatenate([v for v in parts if v is not None], axis=0)
-        pad = lay.padded
-        b_hi, b_lo = split(b)
-        left = jnp.concatenate([m_ref[r, :, k * pad : (k + 1) * pad] for k in range(3)], axis=0)
-        right = jnp.concatenate([b_hi, b_hi, b_lo], axis=0)
-        far = lax.dot_general(left, right, (((0,), (0,)), ((), ())), preferred_element_type=jnp.float32)
-        y = y_ref[r]
-        out_ref[r] = jnp.where(polar_row(band, bands, lay.rows, 2 * p + r), y + far[: lay.segment], y)
+        come = [come_ref[pl.ds(pl.multiple_of(at + 2 * rank * p, 8), 2 * rank), :] for _, _, _, rank, at in lay.peers]
+        finish(2 * p, 0, come)
+        finish(2 * p + 1, 1, come)
 
 
 def local(ring, bands, fields, cutoff):
@@ -278,60 +270,37 @@
     polar = np.abs(2 * row_ids + 1 - total) * 5 > 2 * total
     poles = np.minimum(row_ids, total - 1 - row_ids)
     top = int(1 + (length // 2 - 1) * (2 * poles[polar].max() + 1) // total)
-    table, tiles, ranks = filter_tables(length, segment, top)
+    lines, mixing, bank, ranks = filter_tables(length, segment, top)
     lay = Layout(rows, segment, channels, ring, ranks)
     pad = lay.padded
-    f32 = jnp.float32
+    f32, bf16 = jnp.float32, jnp.bfloat16
     hbm = pl.BlockSpec(memory_space=pltpu.HBM)
-    vmem = pl.BlockSpec(memory_space=pltpu.VMEM)
-    params = functools.partial(pltpu.CompilerParams, vmem_limit_bytes=24 * 1024 * 1024)
-    line, mix, bank = pl.pallas_call(
-        functools.partial(lookup_kernel, lay, top),
-        out_shape=[
-            jax.ShapeDtypeStruct((rows, tiles, LANES), f32),
-            jax.ShapeDtypeStruct((rows, lay.count, LANES), f32),
-            jax.ShapeDtypeStruct((2, (SHAPES + 1) * pad // LANES, LANES), f32),
-        ],
-        in_specs=[pl.BlockSpec(memory_space=pltpu.SMEM), hbm],
-        out_specs=[vmem] * 3,
+    inputs = [pltpu.with_memory_space_constraint(a, pltpu.HBM) for a in (cutoff, fields, *map(jnp.asarray, (lines, mixing, bank)))]
+    return pl.pallas_call(
+        functools.partial(filter_kernel, lay, bands, top),
+        out_shape=jax.ShapeDtypeStruct(fields.shape, fields.dtype),
+        in_specs=[hbm] * 5,
+        out_specs=pl.BlockSpec(memory_space=pltpu.VMEM),
         scratch_shapes=[
-            pltpu.SemaphoreType.DMA,
-            pltpu.SemaphoreType.DMA((rows,)),
-            pltpu.SemaphoreType.DMA((rows,)),
-        ],
-        compiler_params=pltpu.CompilerParams(vmem_limit_bytes=52 * 1024 * 1024),
-        name="lookup",
-    )(cutoff, table)
-    partial, come, left = pl.pallas_call(
-        functools.partial(exchange_kernel, lay, bands, top),
-        out_shape=[
-            jax.ShapeDtypeStruct(fields.shape, f32),
-            jax.ShapeDtypeStruct((lay.total, channels), f32),
-            jax.ShapeDtypeStruct((rows, 2 * lay.count, 3 * pad), jnp.bfloat16),
-        ],
-        in_specs=[pl.BlockSpec(memory_space=pltpu.SMEM), vmem, vmem, vmem, vmem],
-        out_specs=[vmem] * 3,
-        scratch_shapes=[
+            pltpu.SMEM((rows,), jnp.int32),
+            pltpu.VMEM(fields.shape, f32),
+            pltpu.VMEM(lines.shape, f32),
+            pltpu.VMEM(mixing.shape, f32),
+            pltpu.VMEM(bank.shape, f32),
             pltpu.VMEM((lay.total, channels), f32),
-            pltpu.VMEM((rows, 3 * pad, channels), jnp.bfloat16),
-            pltpu.VMEM((2, lay.tall, 3 * pad), jnp.bfloat16),
+            pltpu.VMEM((rows, 2 * lay.count, 3 * pad), bf16),
+            pltpu.VMEM((lay.total, channels), f32),
+            pltpu.VMEM((rows, 3 * pad, channels), bf16),
+            pltpu.VMEM((2, lay.tall, 3 * pad), bf16),
             pltpu.VMEM((4, rows, pad), f32),
+            pltpu.SemaphoreType.DMA((4,)),
+            pltpu.SemaphoreType.DMA((rows // 2,)),
             pltpu.SemaphoreType.DMA((ring - 1, rows // 2)),
             pltpu.SemaphoreType.DMA((ring - 1, rows // 2)),
         ],
-        compiler_params=params(collective_id=0, has_side_effects=True),
-        name="exchange",
-    )(cutoff, fields, line, mix, bank)
-    by_pair = lambda a: pl.BlockSpec((2,) + a.shape[1:], lambda p: (p, 0, 0))
-    return pl.pallas_call(
-        functools.partial(join_kernel, lay, bands),
-        out_shape=jax.ShapeDtypeStruct(fields.shape, fields.dtype),
-        grid=(rows // 2,),
-        in_specs=[by_pair(partial), pl.BlockSpec(come.shape, lambda p: (0, 0)), by_pair(left)],
-        out_specs=by_pair(fields),
-        compiler_params=params(),
-        name="join",
-    )(partial, come, left)
+        compiler_params=pltpu.CompilerParams(collective_id=0, has_side_effects=True, vmem_limit_bytes=48 * 1024 * 1024),
+        name="filter",
+    )(*inputs)
 
 
 def solution(mesh):

time: 19.3 us -> 16.8 us (0.87)
  Pallas kernels: 18 us -> 14.6 us
  local copies, waits for them, and re-layouts: 1.14 us -> 2.09 us
    pallas_call x3 -> x1, Pallas kernels: 18 us -> 14.6 us  [local(): pl.pallas_call(functools.partial(filter_kernel, lay, bands, top), out_sha...]
    unnamed x4 -> x1, local copies, waits for them, and re-layouts: 1.14 us -> 2.09 us
where the time goes in v4:
time: 16.8 us; the launch traced here: 16.7 us
  Pallas kernels  14.6 us (87%)
  local copies, waits for them, and re-layouts  2.09 us (12%)
    pallas_call x1, Pallas kernels, local(): pl.pallas_call(functools.partial(filter_kernel, lay, bands, top), out_sha...  14.6 us
    unnamed x1, local copies, waits for them, and re-layouts  2.09 us

profile of v4, /device:TPU:0, one launch (start us, length us, event | category | flops | bytes accessed | tf_op | source)
XLA Modules:
  0.0 16.7 jit_solution(13695625893419905888)
XLA Ops:
  0.0 14.6 %filter.1 = f32[8,360,384]{2,1,0:T(8,128)S(1)} custom-call(s32[8]{0:T(128)} %cut_hbm.1, f32[8,360,384]{2,1,0:T(8,128)} %x_hbm.1, f32[856,8,128]{2,1,0:T(8,128)} %constant.6.clone.line_hbm, f32[214,24,128]{2,1,0:T(8,128)} %constant.7.clone.mix_hbm, f32[2,16,384]{2,1,0:T(8,128)} %constant.8.clone.bank_hbm), custom_call_target="tpu_custom_call" | custom-call | tf_op jit(solution)/shard_map/filter/pallas_call | solution.py:279
  14.6 2.1 %copy.7 = f32[8,360,384]{2,1,0:T(8,128)} copy(f32[8,360,384]{2,1,0:T(8,128)S(1)} %filter.1) | data formatting | bytes 8847360

commit v5 on v4

--- a/solution.py
+++ b/solution.py
@@ -83,15 +83,14 @@
             here[:, SHAPES] = size[order]
             start += rank
     padded = -(-segment // LANES) * LANES
-    away = np.abs(np.arange(2 * padded) - (padded - 1))
-    tiles = -(-2 * padded // LANES // 8) * 8
-    mirrored = np.zeros((mixing.shape[0] * PER_TILE, tiles * LANES))
-    mirrored[1 : top + 1, : 2 * padded] = lines[:, away]
-    mirrored = mirrored.reshape(-1, tiles, LANES)
+    tiles = padded // LANES
+    halves = np.zeros((-(-(top + 1) // 8) * 8, tiles * LANES))
+    halves[1 : top + 1] = lines[:, : tiles * LANES]
+    halves = halves.reshape(-1, 8 * tiles, LANES)
     banks = np.zeros((2, SHAPES + 1, padded))
     banks[0, :SHAPES, :segment] = shapes.T
     banks[1, :SHAPES, :segment] = shapes[::-1].T
-    return mirrored.astype(np.float32), mixing.astype(np.float32), banks.astype(np.float32), ranks
+    return halves.astype(np.float32), mixing.astype(np.float32), banks.astype(np.float32), ranks
 
 
 def split(a):
@@ -130,9 +129,9 @@
     return hi, mid, (rest - mid.astype(jnp.float32)).astype(jnp.bfloat16)
 
 
-def filter_kernel(lay, bands, top, cut_hbm, x_hbm, line_hbm, mix_hbm, bank_hbm, y_ref, cut_ref, x_ref, line_ref, mix_ref, bank_ref, come_ref, m_ref, send, xs, left, turns, load_sem, x_sem, send_sem, recv_sem):
+def filter_kernel(lay, bands, top, cut_hbm, x_hbm, line_hbm, mix_hbm, bank_hbm, y_ref, cut_ref, x_ref, line_ref, mix_ref, bank_ref, come_ref, m_ref, send, xs, left, turns, both, load_sem, x_sem, send_sem, recv_sem):
     seg, pad, ring, pairs = lay.segment, lay.padded, lay.ring, lay.rows // 2
-    length = seg * ring
+    length, tops = seg * ring, 2 * lay.count
     band, me = lax.axis_index("lat"), lax.axis_index("lon")
     barrier = pltpu.get_barrier_semaphore()
 
@@ -157,9 +156,7 @@
     ]
     for copy in loads[:3]:
         copy.start()
-    for p in range(pairs):
-        fetch(p).start()
-    loads[3].start()
+    fetch(0).start()
     for step in range(1, ring):
         pl.semaphore_signal(barrier, inc=1, device_id={"lon": lax.rem(me + step, ring)}, device_id_type=MESH)
 
@@ -182,8 +179,10 @@
     slot = lax.broadcasted_iota(jnp.int32, (lay.count, LANES), 1)
     loads[1].wait()
     loads[2].wait()
-
-    def project(i):
+    for copy in [fetch(1), loads[3]] + [fetch(p) for p in range(2, pairs)]:
+        copy.start()
+
+    def mixed(i):
         x = x_ref[i]
         hi, lo = split(x)
         xs[i, 0:seg] = hi
@@ -203,22 +202,62 @@
         hi, lo = split(jnp.concatenate([q[:, :pad], q[:, pad:] * size], axis=0))
         m = jnp.concatenate([hi, lo, hi], axis=1)
         m_ref[i] = m
-        return jnp.dot(m, xs[i], preferred_element_type=jnp.float32)
-
-    def diagonal(i, s):
-        line = line_ref[jnp.clip(cut_ref[i], 1, top)]
-        line = jnp.concatenate([jnp.broadcast_to(line[k : k + 1], (LANES, LANES)) for k in range(2 * pad // LANES)], axis=1)
-        sheet = pltpu.roll(line, 2 * pad - (LANES - 1), 1, stride=1, stride_axis=0)[:, : 2 * pad - LANES]
+        return m
+
+    def mirror():
+        tiles = pad // LANES
+        rows = []
+        for i in range(lay.rows):
+            cut = jnp.clip(cut_ref[i], 1, top)
+            rows += [line_ref[cut // 8, pl.ds(lax.rem(cut, 8) * tiles + k, 1), :] for k in range(tiles)]
+        ahead = jnp.concatenate(rows, axis=0)
+        count = ahead.shape[0]
+        lane = lax.broadcasted_iota(jnp.int32, (LANES, LANES), 0) + lax.broadcasted_iota(jnp.int32, (LANES, LANES), 1)
+        turn = (lane == LANES).astype(jnp.bfloat16)
+        back = jnp.dot(jnp.concatenate(three(ahead), axis=0), turn, preferred_element_type=jnp.float32)
+        back = back[:count] + back[count : 2 * count] + back[2 * count :]
+        ahead_next = jnp.concatenate([ahead[1:], ahead[:1]], axis=0)
+        back = jnp.where(lax.broadcasted_iota(jnp.int32, back.shape, 1) == 0, ahead_next, back)
+        for i in range(lay.rows):
+            for k in range(tiles):
+                at = i * tiles + k
+                both[pl.ds(i, 1), (tiles - 1 - k) * LANES : (tiles - k) * LANES] = back[at : at + 1]
+                both[pl.ds(i, 1), (tiles + k) * LANES : (tiles + k + 1) * LANES] = ahead[at : at + 1]
+
+    def toeplitz(i, s):
+        line = jnp.broadcast_to(both[pl.ds(i, 1), :], (LANES, 2 * pad))
+        sheet = pltpu.roll(line, 2 * pad - LANES, 1, stride=1, stride_axis=0)[:, : 2 * pad - LANES]
         hi, lo = split(sheet)
         for q in range(pad // LANES):
             cols = slice(pad - LANES * (q + 1), 2 * pad - LANES * (q + 1))
             rows = min(LANES, lay.tall - q * LANES)
-            block = slice(q * LANES, q * LANES + rows)
+            block = slice(tops + q * LANES, tops + q * LANES + rows)
             left[s, block, 0:pad] = hi[:rows, cols]
             left[s, block, pad : 2 * pad] = lo[:rows, cols]
             left[s, block, 2 * pad : 3 * pad] = hi[:rows, cols]
-        y = jnp.dot(left[s], xs[i], preferred_element_type=jnp.float32)[:seg]
-        y_ref[i] = y
+
+    def keep(i, y):
+        on = polar_row(band, bands, lay.rows, i)
+
+        @pl.when(on)
+        def _():
+            y_ref[i] = y
+
+        @pl.when(jnp.logical_not(on))
+        def _():
+            y_ref[i] = x_ref[i]
+
+    def stacked(i, s):
+        left[s, 0:tops] = mixed(i)
+        toeplitz(i, s)
+        y = jnp.dot(left[s], xs[i], preferred_element_type=jnp.float32)
+        keep(i, y[tops : tops + seg])
+        return y[:tops]
+
+    def post(p, first, second):
+        for _, at_row, _, rank, at in lay.peers:
+            two = jnp.concatenate([first[at_row : at_row + rank], second[at_row : at_row + rank]], axis=0)
+            send[pl.ds(pl.multiple_of(at + 2 * rank * p, 8), 2 * rank), :] = two
 
     def finish(i, r, come):
         parts = [None] * (2 * lay.count)
@@ -230,29 +269,29 @@
         right = jnp.concatenate([hi, hi, lo], axis=0)
         wide = jnp.concatenate([m_ref[i, :, k * pad : (k + 1) * pad] for k in range(3)], axis=0)
         far = lax.dot_general(wide, right, (((0,), (0,)), ((), ())), preferred_element_type=jnp.float32)[:seg]
-        y_ref[i] = jnp.where(polar_row(band, bands, lay.rows, i), y_ref[i] + far, x_ref[i])
-
-    @pl.loop(0, pairs)
+
+        @pl.when(polar_row(band, bands, lay.rows, i))
+        def _():
+            y_ref[i] += far
+
+    fetch(0).wait()
+    post(0, *[jnp.dot(mixed(i), xs[i], preferred_element_type=jnp.float32) for i in range(2)])
+    pl.semaphore_wait(barrier, ring - 1)
+    for n in range(ring - 1):
+        push(n, 0).start()
+    loads[3].wait()
+    mirror()
+
+    @pl.loop(1, pairs)
     def _(p):
         fetch(p).wait()
-        first, second = project(2 * p), project(2 * p + 1)
-        for _, at_row, _, rank, at in lay.peers:
-            both = jnp.concatenate([first[at_row : at_row + rank], second[at_row : at_row + rank]], axis=0)
-            send[pl.ds(pl.multiple_of(at + 2 * rank * p, 8), 2 * rank), :] = both
-
-        @pl.when(p == 0)
-        def _():
-            pl.semaphore_wait(barrier, ring - 1)
-
+        post(p, stacked(2 * p, 0), stacked(2 * p + 1, 1))
         for n in range(ring - 1):
             push(n, p).start()
 
-    loads[3].wait()
-
-    @pl.loop(0, pairs)
-    def _(p):
-        diagonal(2 * p, 0)
-        diagonal(2 * p + 1, 1)
+    for i in range(2):
+        toeplitz(i, i)
+        keep(i, jnp.dot(left[i, tops:], xs[i], preferred_element_type=jnp.float32)[:seg])
 
     @pl.loop(0, pairs)
     def _(p):
@@ -291,8 +330,9 @@
             pltpu.VMEM((rows, 2 * lay.count, 3 * pad), bf16),
             pltpu.VMEM((lay.total, channels), f32),
             pltpu.VMEM((rows, 3 * pad, channels), bf16),
-            pltpu.VMEM((2, lay.tall, 3 * pad), bf16),
+            pltpu.VMEM((2, -(-2 * lay.count // 16) * 16 + lay.tall, 3 * pad), bf16),
             pltpu.VMEM((4, rows, pad), f32),
+            pltpu.VMEM((rows, 2 * pad), f32),
             pltpu.SemaphoreType.DMA((4,)),
             pltpu.SemaphoreType.DMA((rows // 2,)),
             pltpu.SemaphoreType.DMA((ring - 1, rows // 2)),

time: 16.8 us -> 19.6 us (1.17)
  Pallas kernels: 14.6 us -> 17.3 us
    pallas_call x1, Pallas kernels: 14.6 us -> 17.3 us  [local(): pl.pallas_call(functools.partial(filter_kernel, lay, bands, top), out_sha...]
where the time goes in v5:
time: 19.6 us; the launch traced here: 19.4 us
  Pallas kernels  17.3 us (88%)
  local copies, waits for them, and re-layouts  2.09 us (11%)
    pallas_call x1, Pallas kernels, local(): pl.pallas_call(functools.partial(filter_kernel, lay, bands, top), out_sha...  17.3 us
    unnamed x1, local copies, waits for them, and re-layouts  2.09 us

profile of v5, /device:TPU:0, one launch (start us, length us, event | category | flops | bytes accessed | tf_op | source)
XLA Modules:
  0.0 19.4 jit_solution(3534575036449226217)
XLA Ops:
  0.0 17.3 %filter.1 = f32[8,360,384]{2,1,0:T(8,128)S(1)} custom-call(s32[8]{0:T(128)} %cut_hbm.1, f32[8,360,384]{2,1,0:T(8,128)} %x_hbm.1, f32[107,24,128]{2,1,0:T(8,128)} %constant.6.clone.line_hbm, f32[214,24,128]{2,1,0:T(8,128)} %constant.7.clone.mix_hbm, f32[2,16,384]{2,1,0:T(8,128)} %constant.8.clone.bank_hbm), custom_call_target="tpu_custom_call" | custom-call | tf_op jit(solution)/shard_map/filter/pallas_call | solution.py:318
  17.3 2.1 %copy.7 = f32[8,360,384]{2,1,0:T(8,128)} copy(f32[8,360,384]{2,1,0:T(8,128)S(1)} %filter.1) | data formatting | bytes 8847360

commit v6 on v5

--- a/solution.py
+++ b/solution.py
@@ -131,9 +131,12 @@
 
 def filter_kernel(lay, bands, top, cut_hbm, x_hbm, line_hbm, mix_hbm, bank_hbm, y_ref, cut_ref, x_ref, line_ref, mix_ref, bank_ref, come_ref, m_ref, send, xs, left, turns, both, load_sem, x_sem, send_sem, recv_sem):
     seg, pad, ring, pairs = lay.segment, lay.padded, lay.ring, lay.rows // 2
-    length, tops = seg * ring, 2 * lay.count
+    length = seg * ring
     band, me = lax.axis_index("lat"), lax.axis_index("lon")
     barrier = pltpu.get_barrier_semaphore()
+    total = lay.rows * bands
+    polar = [abs(2 * i + 1 - total) * 5 > 2 * total for i in range(total)]
+    mixed_pairs = polar[0::2] != polar[1::2]
 
     def push(n, p):
         step, _, _, rank, at = lay.peers[n]
@@ -165,6 +168,8 @@
             for k in range(3):
                 xs[r, k * pad + seg : (k + 1) * pad] = jnp.zeros((pad - seg, lay.channels), jnp.bfloat16)
     loads[0].wait()
+    for copy in [fetch(1), loads[3]] + [fetch(p) for p in range(2, pairs)]:
+        copy.start()
     row = lax.broadcasted_iota(jnp.int32, (lay.rows, pad), 0)
     spot = lax.broadcasted_iota(jnp.int32, (lay.rows, pad), 1).astype(jnp.float32)
     cut = jnp.zeros((lay.rows, pad), jnp.float32)
@@ -179,8 +184,6 @@
     slot = lax.broadcasted_iota(jnp.int32, (lay.count, LANES), 1)
     loads[1].wait()
     loads[2].wait()
-    for copy in [fetch(1), loads[3]] + [fetch(p) for p in range(2, pairs)]:
-        copy.start()
 
     def mixed(i):
         x = x_ref[i]
@@ -231,28 +234,10 @@
         for q in range(pad // LANES):
             cols = slice(pad - LANES * (q + 1), 2 * pad - LANES * (q + 1))
             rows = min(LANES, lay.tall - q * LANES)
-            block = slice(tops + q * LANES, tops + q * LANES + rows)
+            block = slice(q * LANES, q * LANES + rows)
             left[s, block, 0:pad] = hi[:rows, cols]
             left[s, block, pad : 2 * pad] = lo[:rows, cols]
             left[s, block, 2 * pad : 3 * pad] = hi[:rows, cols]
-
-    def keep(i, y):
-        on = polar_row(band, bands, lay.rows, i)
-
-        @pl.when(on)
-        def _():
-            y_ref[i] = y
-
-        @pl.when(jnp.logical_not(on))
-        def _():
-            y_ref[i] = x_ref[i]
-
-    def stacked(i, s):
-        left[s, 0:tops] = mixed(i)
-        toeplitz(i, s)
-        y = jnp.dot(left[s], xs[i], preferred_element_type=jnp.float32)
-        keep(i, y[tops : tops + seg])
-        return y[:tops]
 
     def post(p, first, second):
         for _, at_row, _, rank, at in lay.peers:
@@ -269,37 +254,45 @@
         right = jnp.concatenate([hi, hi, lo], axis=0)
         wide = jnp.concatenate([m_ref[i, :, k * pad : (k + 1) * pad] for k in range(3)], axis=0)
         far = lax.dot_general(wide, right, (((0,), (0,)), ((), ())), preferred_element_type=jnp.float32)[:seg]
-
-        @pl.when(polar_row(band, bands, lay.rows, i))
+        y = y_ref[i] + far
+        y_ref[i] = jnp.where(polar_row(band, bands, lay.rows, i), y, x_ref[i]) if mixed_pairs else y
+
+    @pl.loop(0, pairs)
+    def _(p):
+        fetch(p).wait()
+        post(p, *[jnp.dot(mixed(2 * p + r), xs[2 * p + r], preferred_element_type=jnp.float32) for r in range(2)])
+
+        @pl.when(p == 0)
         def _():
-            y_ref[i] += far
-
-    fetch(0).wait()
-    post(0, *[jnp.dot(mixed(i), xs[i], preferred_element_type=jnp.float32) for i in range(2)])
-    pl.semaphore_wait(barrier, ring - 1)
-    for n in range(ring - 1):
-        push(n, 0).start()
+            pl.semaphore_wait(barrier, ring - 1)
+
+        for n in range(ring - 1):
+            push(n, p).start()
+
     loads[3].wait()
     mirror()
 
-    @pl.loop(1, pairs)
+    @pl.loop(0, pairs)
     def _(p):
-        fetch(p).wait()
-        post(p, stacked(2 * p, 0), stacked(2 * p + 1, 1))
-        for n in range(ring - 1):
-            push(n, p).start()
-
-    for i in range(2):
-        toeplitz(i, i)
-        keep(i, jnp.dot(left[i, tops:], xs[i], preferred_element_type=jnp.float32)[:seg])
+        for r in range(2):
+            toeplitz(2 * p + r, r)
+            y_ref[2 * p + r] = jnp.dot(left[r], xs[2 * p + r], preferred_element_type=jnp.float32)[:seg]
 
     @pl.loop(0, pairs)
     def _(p):
         for n in range(ring - 1):
             push(n, p).wait()
-        come = [come_ref[pl.ds(pl.multiple_of(at + 2 * rank * p, 8), 2 * rank), :] for _, _, _, rank, at in lay.peers]
-        finish(2 * p, 0, come)
-        finish(2 * p + 1, 1, come)
+        any_on = jnp.logical_or(polar_row(band, bands, lay.rows, 2 * p), polar_row(band, bands, lay.rows, 2 * p + 1))
+
+        @pl.when(any_on)
+        def _():
+            come = [come_ref[pl.ds(pl.multiple_of(at + 2 * rank * p, 8), 2 * rank), :] for _, _, _, rank, at in lay.peers]
+            finish(2 * p, 0, come)
+            finish(2 * p + 1, 1, come)
+
+        @pl.when(jnp.logical_not(any_on))
+        def _():
+            y_ref[pl.ds(2 * p, 2)] = x_ref[pl.ds(2 * p, 2)]
 
 
 def local(ring, bands, fields, cutoff):
@@ -330,7 +323,7 @@
             pltpu.VMEM((rows, 2 * lay.count, 3 * pad), bf16),
             pltpu.VMEM((lay.total, channels), f32),
             pltpu.VMEM((rows, 3 * pad, channels), bf16),
-            pltpu.VMEM((2, -(-2 * lay.count // 16) * 16 + lay.tall, 3 * pad), bf16),
+            pltpu.VMEM((2, lay.tall, 3 * pad), bf16),
             pltpu.VMEM((4, rows, pad), f32),
             pltpu.VMEM((rows, 2 * pad), f32),
             pltpu.SemaphoreType.DMA((4,)),

time: 19.6 us -> 16.5 us (0.84)
  Pallas kernels: 17.3 us -> 14.2 us
    pallas_call x1, Pallas kernels: 17.3 us -> 14.2 us  [local(): pl.pallas_call(functools.partial(filter_kernel, lay, bands, top), out_sha...]
where the time goes in v6:
time: 16.5 us; the launch traced here: 16.3 us
  Pallas kernels  14.2 us (86%)
  local copies, waits for them, and re-layouts  2.09 us (13%)
    pallas_call x1, Pallas kernels, local(): pl.pallas_call(functools.partial(filter_kernel, lay, bands, top), out_sha...  14.2 us
    unnamed x1, local copies, waits for them, and re-layouts  2.09 us

profile of v6, /device:TPU:0, one launch (start us, length us, event | category | flops | bytes accessed | tf_op | source)
XLA Modules:
  0.0 16.3 jit_solution(7369026284736887751)
XLA Ops:
  0.0 14.2 %filter.1 = f32[8,360,384]{2,1,0:T(8,128)S(1)} custom-call(s32[8]{0:T(128)} %cut_hbm.1, f32[8,360,384]{2,1,0:T(8,128)} %x_hbm.1, f32[107,24,128]{2,1,0:T(8,128)} %constant.6.clone.line_hbm, f32[214,24,128]{2,1,0:T(8,128)} %constant.7.clone.mix_hbm, f32[2,16,384]{2,1,0:T(8,128)} %constant.8.clone.bank_hbm), custom_call_target="tpu_custom_call" | custom-call | tf_op jit(solution)/shard_map/filter/pallas_call | solution.py:311
  14.2 2.1 %copy.7 = f32[8,360,384]{2,1,0:T(8,128)} copy(f32[8,360,384]{2,1,0:T(8,128)S(1)} %filter.1) | data formatting | bytes 8847360

commit v7 on v6

--- a/solution.py
+++ b/solution.py
@@ -90,7 +90,9 @@
     banks = np.zeros((2, SHAPES + 1, padded))
     banks[0, :SHAPES, :segment] = shapes.T
     banks[1, :SHAPES, :segment] = shapes[::-1].T
-    return halves.astype(np.float32), mixing.astype(np.float32), banks.astype(np.float32), ranks
+    near = np.concatenate([mixing[:, :NEAR_RANK], np.zeros((mixing.shape[0] % 2, NEAR_RANK, LANES))], axis=0)
+    near = near.reshape(-1, 2 * NEAR_RANK, LANES)
+    return [a.astype(np.float32) for a in (halves, near, mixing[:, NEAR_RANK:], banks)], ranks
 
 
 def split(a):
@@ -113,12 +115,19 @@
         self.ranks = ranks
         self.count = sum(ranks)
         starts = np.concatenate([[0], np.cumsum(ranks)]).astype(int)
-        plus = [(d, self.count + starts[d - 1], starts[d - 1], ranks[d - 1]) for d in range(1, self.half + 1)]
-        minus = [(ring - d, starts[d - 1], self.count + starts[d - 1], ranks[d - 1]) for d in range(1, self.half)]
+        self.far = self.count - NEAR_RANK
+
+        def row(d, flip):
+            return NEAR_RANK * flip if d == 1 else int(2 * NEAR_RANK + self.far * flip + starts[d - 1] - NEAR_RANK)
+
+        self.unused = row(self.half, 1)
+        plus = [(d, row(d, 1), row(d, 0), ranks[d - 1], d == 1) for d in range(1, self.half + 1)]
+        minus = [(ring - d, row(d, 0), row(d, 1), ranks[d - 1], d == 1) for d in range(1, self.half)]
         self.peers, at = [], 0
-        for step, send_row, come_row, rank in plus + minus:
-            self.peers.append((step, int(send_row), int(come_row), rank, at))
+        for step, send_row, come_row, rank, near in sorted(plus + minus, key=lambda peer: not peer[4]):
+            self.peers.append((step, send_row, come_row, rank, at))
             at += rank * rows
+        self.close = sum(peer[4] for peer in plus + minus)
         self.total = at
 
 
@@ -129,7 +138,7 @@
     return hi, mid, (rest - mid.astype(jnp.float32)).astype(jnp.bfloat16)
 
 
-def filter_kernel(lay, bands, top, cut_hbm, x_hbm, line_hbm, mix_hbm, bank_hbm, y_ref, cut_ref, x_ref, line_ref, mix_ref, bank_ref, come_ref, m_ref, send, xs, left, turns, both, load_sem, x_sem, send_sem, recv_sem):
+def filter_kernel(lay, bands, top, cut_hbm, x_hbm, line_hbm, near_hbm, far_hbm, bank_hbm, y_ref, cut_ref, x_ref, line_ref, near_ref, far_ref, bank_ref, come_ref, m_ref, send, xs, left, turns, both, mt_ref, load_sem, x_sem, send_sem, recv_sem):
     seg, pad, ring, pairs = lay.segment, lay.padded, lay.ring, lay.rows // 2
     length = seg * ring
     band, me = lax.axis_index("lat"), lax.axis_index("lon")
@@ -155,11 +164,10 @@
 
     loads = [
         pltpu.make_async_copy(a, b, load_sem.at[k])
-        for k, (a, b) in enumerate(((cut_hbm, cut_ref), (bank_hbm, bank_ref), (mix_hbm, mix_ref), (line_hbm, line_ref)))
+        for k, (a, b) in enumerate(((cut_hbm, cut_ref), (bank_hbm, bank_ref), (near_hbm, near_ref), (line_hbm, line_ref), (far_hbm, far_ref)))
     ]
-    for copy in loads[:3]:
+    for copy in loads[:3] + [fetch(0), loads[4]]:
         copy.start()
-    fetch(0).start()
     for step in range(1, ring):
         pl.semaphore_signal(barrier, inc=1, device_id={"lon": lax.rem(me + step, ring)}, device_id_type=MESH)
 
@@ -181,31 +189,44 @@
         angle = turn * (2.0 * np.pi / length)
         turns[2 * f] = jnp.cos(angle)
         turns[2 * f + 1] = jnp.sin(angle)
-    slot = lax.broadcasted_iota(jnp.int32, (lay.count, LANES), 1)
-    loads[1].wait()
-    loads[2].wait()
-
-    def mixed(i):
-        x = x_ref[i]
-        hi, lo = split(x)
+    def halve(i):
+        hi, lo = split(x_ref[i])
         xs[i, 0:seg] = hi
         xs[i, pad : pad + seg] = hi
         xs[i, 2 * pad : 2 * pad + seg] = lo
+
+    def weights(i, far):
+        cut = jnp.clip(cut_ref[i], 1, top)
+        if far:
+            mix = far_ref[cut // PER_TILE]
+        else:
+            mix = near_ref[cut // (2 * PER_TILE)]
+            mix = jnp.where(lax.rem(cut // PER_TILE, 2) == 1, mix[NEAR_RANK:], mix[:NEAR_RANK])
+        slot = lax.broadcasted_iota(jnp.int32, mix.shape, 1)
+        mix = jnp.where(slot // SLOT == lax.rem(cut, PER_TILE), mix, 0.0)
+        size = jnp.sum(jnp.where(lax.rem(slot, SLOT) == SHAPES, mix, 0.0), axis=1, keepdims=True)
+        return functools.reduce(jnp.add, [mix[:, k * SLOT : (k + 1) * SLOT] for k in range(PER_TILE)]), size
+
+    def project(i, parts):
         basis = []
         for f in range(2):
             basis.append(jnp.concatenate([bank_ref[f] * turns[2 * f + w, pl.ds(i, 1), :] for w in range(2)], axis=0))
         hi, mid, lo = three(jnp.concatenate(basis, axis=1))
         right = jnp.concatenate([hi, mid, lo, hi, mid, hi], axis=0)
-        cut = jnp.clip(cut_ref[i], 1, top)
-        mix = jnp.where(slot // SLOT == lax.rem(cut, PER_TILE), mix_ref[cut // PER_TILE], 0.0)
-        size = jnp.sum(jnp.where(lax.rem(slot, SLOT) == SHAPES, mix, 0.0), axis=1, keepdims=True)
-        mix = functools.reduce(jnp.add, [mix[:, k * SLOT : (k + 1) * SLOT] for k in range(PER_TILE)])
-        hi, mid, lo = three(mix)
+        both_weights = [weights(i, far) for far in parts]
+        hi, mid, lo = three(jnp.concatenate([w for w, _ in both_weights], axis=0))
         q = jnp.dot(jnp.concatenate([hi, hi, hi, mid, mid, lo], axis=1), right, preferred_element_type=jnp.float32)
-        hi, lo = split(jnp.concatenate([q[:, :pad], q[:, pad:] * size], axis=0))
-        m = jnp.concatenate([hi, lo, hi], axis=1)
-        m_ref[i] = m
-        return m
+        rows, at = [], 0
+        for _, size in both_weights:
+            part = q[at : at + size.shape[0]]
+            rows += [part[:, :pad], part[:, pad:] * size]
+            at += size.shape[0]
+        hi, lo = split(jnp.concatenate(rows, axis=0))
+        start, tops = (2 * NEAR_RANK if parts[0] else 0), 2 * at
+        for k, part in enumerate((hi, lo, hi)):
+            m_ref[i, start : start + tops, k * pad : (k + 1) * pad] = part
+        two = jnp.dot(jnp.concatenate([hi, lo], axis=0), xs[i, :pad], preferred_element_type=jnp.float32)
+        return two[:tops] + two[tops:] + jnp.dot(hi, xs[i, 2 * pad :], preferred_element_type=jnp.float32)
 
     def mirror():
         tiles = pad // LANES
@@ -239,44 +260,56 @@
             left[s, block, pad : 2 * pad] = lo[:rows, cols]
             left[s, block, 2 * pad : 3 * pad] = hi[:rows, cols]
 
-    def post(p, first, second):
-        for _, at_row, _, rank, at in lay.peers:
-            two = jnp.concatenate([first[at_row : at_row + rank], second[at_row : at_row + rank]], axis=0)
+    def post(p, parts):
+        first, second = [project(2 * p + r, parts) for r in range(2)]
+        which = range(0 if not parts[0] else lay.close, ring - 1 if parts[-1] else lay.close)
+        shift = 2 * NEAR_RANK if parts[0] else 0
+        for n in which:
+            _, row, _, rank, at = lay.peers[n]
+            row = row - shift
+            two = jnp.concatenate([first[row : row + rank], second[row : row + rank]], axis=0)
             send[pl.ds(pl.multiple_of(at + 2 * rank * p, 8), 2 * rank), :] = two
+        return which
 
     def finish(i, r, come):
         parts = [None] * (2 * lay.count)
         for (_, _, at_row, rank, _), both in zip(lay.peers, come):
             parts[at_row] = both[r * rank : (r + 1) * rank]
-        unused = lay.count + sum(lay.ranks[:-1])
-        parts[unused] = jnp.zeros((lay.ranks[-1], lay.channels), jnp.float32)
+        parts[lay.unused] = jnp.zeros((lay.ranks[-1], lay.channels), jnp.float32)
         hi, lo = split(jnp.concatenate([v for v in parts if v is not None], axis=0))
         right = jnp.concatenate([hi, hi, lo], axis=0)
-        wide = jnp.concatenate([m_ref[i, :, k * pad : (k + 1) * pad] for k in range(3)], axis=0)
-        far = lax.dot_general(wide, right, (((0,), (0,)), ((), ())), preferred_element_type=jnp.float32)[:seg]
+        far = jnp.dot(mt_ref[i], right, preferred_element_type=jnp.float32)[:seg]
         y = y_ref[i] + far
         y_ref[i] = jnp.where(polar_row(band, bands, lay.rows, i), y, x_ref[i]) if mixed_pairs else y
 
-    @pl.loop(0, pairs)
+    loads[1].wait()
+    loads[2].wait()
+    fetch(0).wait()
+    halve(0)
+    halve(1)
+    close = post(0, (0,))
+    pl.semaphore_wait(barrier, ring - 1)
+    for n in close:
+        push(n, 0).start()
+    loads[4].wait()
+    for n in post(0, (1,)):
+        push(n, 0).start()
+
+    @pl.loop(1, pairs)
     def _(p):
         fetch(p).wait()
-        post(p, *[jnp.dot(mixed(2 * p + r), xs[2 * p + r], preferred_element_type=jnp.float32) for r in range(2)])
-
-        @pl.when(p == 0)
-        def _():
-            pl.semaphore_wait(barrier, ring - 1)
-
-        for n in range(ring - 1):
+        halve(2 * p)
+        halve(2 * p + 1)
+        for n in post(p, (0, 1)):
             push(n, p).start()
 
     loads[3].wait()
     mirror()
 
-    @pl.loop(0, pairs)
-    def _(p):
-        for r in range(2):
-            toeplitz(2 * p + r, r)
-            y_ref[2 * p + r] = jnp.dot(left[r], xs[2 * p + r], preferred_element_type=jnp.float32)[:seg]
+    for i in range(lay.rows):
+        toeplitz(i, i % 2)
+        mt_ref[i] = jnp.concatenate([m_ref[i, :, k * pad : (k + 1) * pad] for k in range(3)], axis=0).T
+        y_ref[i] = jnp.dot(left[i % 2], xs[i], preferred_element_type=jnp.float32)[:seg]
 
     @pl.loop(0, pairs)
     def _(p):
@@ -302,23 +335,21 @@
     polar = np.abs(2 * row_ids + 1 - total) * 5 > 2 * total
     poles = np.minimum(row_ids, total - 1 - row_ids)
     top = int(1 + (length // 2 - 1) * (2 * poles[polar].max() + 1) // total)
-    lines, mixing, bank, ranks = filter_tables(length, segment, top)
+    tables, ranks = filter_tables(length, segment, top)
     lay = Layout(rows, segment, channels, ring, ranks)
     pad = lay.padded
     f32, bf16 = jnp.float32, jnp.bfloat16
     hbm = pl.BlockSpec(memory_space=pltpu.HBM)
-    inputs = [pltpu.with_memory_space_constraint(a, pltpu.HBM) for a in (cutoff, fields, *map(jnp.asarray, (lines, mixing, bank)))]
+    inputs = [pltpu.with_memory_space_constraint(a, pltpu.HBM) for a in (cutoff, fields, *map(jnp.asarray, tables))]
     return pl.pallas_call(
         functools.partial(filter_kernel, lay, bands, top),
         out_shape=jax.ShapeDtypeStruct(fields.shape, fields.dtype),
-        in_specs=[hbm] * 5,
+        in_specs=[hbm] * 6,
         out_specs=pl.BlockSpec(memory_space=pltpu.VMEM),
         scratch_shapes=[
             pltpu.SMEM((rows,), jnp.int32),
             pltpu.VMEM(fields.shape, f32),
-            pltpu.VMEM(lines.shape, f32),
-            pltpu.VMEM(mixing.shape, f32),
-            pltpu.VMEM(bank.shape, f32),
+            *[pltpu.VMEM(a.shape, f32) for a in tables],
             pltpu.VMEM((lay.total, channels), f32),
             pltpu.VMEM((rows, 2 * lay.count, 3 * pad), bf16),
             pltpu.VMEM((lay.total, channels), f32),
@@ -326,7 +357,8 @@
             pltpu.VMEM((2, lay.tall, 3 * pad), bf16),
             pltpu.VMEM((4, rows, pad), f32),
             pltpu.VMEM((rows, 2 * pad), f32),
-            pltpu.SemaphoreType.DMA((4,)),
+            pltpu.VMEM((rows, pad, 6 * lay.count), bf16),
+            pltpu.SemaphoreType.DMA((5,)),
             pltpu.SemaphoreType.DMA((rows // 2,)),
             pltpu.SemaphoreType.DMA((ring - 1, rows // 2)),
             pltpu.SemaphoreType.DMA((ring - 1, rows // 2)),

time: 16.5 us -> 16.7 us (1.012)
  Pallas kernels: 14.2 us -> 14.4 us
    pallas_call x1, Pallas kernels: 14.2 us -> 14.4 us  [local(): pl.pallas_call(functools.partial(filter_kernel, lay, bands, top), out_sha...]
where the time goes in v7:
time: 16.7 us; the launch traced here: 16.5 us
  Pallas kernels  14.4 us (86%)
  local copies, waits for them, and re-layouts  2.09 us (13%)
    pallas_call x1, Pallas kernels, local(): pl.pallas_call(functools.partial(filter_kernel, lay, bands, top), out_sha...  14.4 us
    unnamed x1, local copies, waits for them, and re-layouts  2.09 us

profile of v7, /device:TPU:0, one launch (start us, length us, event | category | flops | bytes accessed | tf_op | source)
XLA Modules:
  0.0 16.5 jit_solution(8175159801180490027)
XLA Ops:
  0.0 14.4 %filter.1 = f32[8,360,384]{2,1,0:T(8,128)S(1)} custom-call(s32[8]{0:T(128)} %cut_hbm.1, f32[8,360,384]{2,1,0:T(8,128)} %x_hbm.1, f32[107,24,128]{2,1,0:T(8,128)} %constant.8.clone.line_hbm, f32[107,24,128]{2,1,0:T(8,128)} %constant.9.clone.near_hbm, f32[214,12,128]{2,1,0:T(8,128)} %constant.10.clone.far_hbm, f32[2,16,384]{2,1,0:T(8,128)} %constant.11.clone.bank_hbm), custom_call_target="tpu_custom_call" | custom-call | tf_op jit(solution)/shard_map/filter/pallas_call | solution.py:344
  14.4 2.1 %copy.8 = f32[8,360,384]{2,1,0:T(8,128)} copy(f32[8,360,384]{2,1,0:T(8,128)S(1)} %filter.1) | data formatting | bytes 8847360

commit v8 on v6

--- a/solution.py
+++ b/solution.py
@@ -129,7 +129,7 @@
     return hi, mid, (rest - mid.astype(jnp.float32)).astype(jnp.bfloat16)
 
 
-def filter_kernel(lay, bands, top, cut_hbm, x_hbm, line_hbm, mix_hbm, bank_hbm, y_ref, cut_ref, x_ref, line_ref, mix_ref, bank_ref, come_ref, m_ref, send, xs, left, turns, both, load_sem, x_sem, send_sem, recv_sem):
+def filter_kernel(lay, bands, top, cut_hbm, x_hbm, line_hbm, mix_hbm, bank_hbm, y_ref, cut_ref, x_ref, line_ref, mix_ref, bank_ref, come_ref, m_ref, send, xs, left, turns, both, mt_ref, load_sem, x_sem, send_sem, recv_sem):
     seg, pad, ring, pairs = lay.segment, lay.padded, lay.ring, lay.rows // 2
     length = seg * ring
     band, me = lax.axis_index("lat"), lax.axis_index("lon")
@@ -207,6 +207,12 @@
         m_ref[i] = m
         return m
 
+    def project(i):
+        m = mixed(i)
+        tops = 2 * lay.count
+        two = jnp.dot(jnp.concatenate([m[:, :pad], m[:, pad : 2 * pad]], axis=0), xs[i, :pad], preferred_element_type=jnp.float32)
+        return two[:tops] + two[tops:] + jnp.dot(m[:, :pad], xs[i, 2 * pad :], preferred_element_type=jnp.float32)
+
     def mirror():
         tiles = pad // LANES
         rows = []
@@ -252,15 +258,14 @@
         parts[unused] = jnp.zeros((lay.ranks[-1], lay.channels), jnp.float32)
         hi, lo = split(jnp.concatenate([v for v in parts if v is not None], axis=0))
         right = jnp.concatenate([hi, hi, lo], axis=0)
-        wide = jnp.concatenate([m_ref[i, :, k * pad : (k + 1) * pad] for k in range(3)], axis=0)
-        far = lax.dot_general(wide, right, (((0,), (0,)), ((), ())), preferred_element_type=jnp.float32)[:seg]
+        far = jnp.dot(mt_ref[i], right, preferred_element_type=jnp.float32)[:seg]
         y = y_ref[i] + far
         y_ref[i] = jnp.where(polar_row(band, bands, lay.rows, i), y, x_ref[i]) if mixed_pairs else y
 
     @pl.loop(0, pairs)
     def _(p):
         fetch(p).wait()
-        post(p, *[jnp.dot(mixed(2 * p + r), xs[2 * p + r], preferred_element_type=jnp.float32) for r in range(2)])
+        post(p, *[project(2 * p + r) for r in range(2)])
 
         @pl.when(p == 0)
         def _():
@@ -272,11 +277,10 @@
     loads[3].wait()
     mirror()
 
-    @pl.loop(0, pairs)
-    def _(p):
-        for r in range(2):
-            toeplitz(2 * p + r, r)
-            y_ref[2 * p + r] = jnp.dot(left[r], xs[2 * p + r], preferred_element_type=jnp.float32)[:seg]
+    for i in range(lay.rows):
+        toeplitz(i, i % 2)
+        mt_ref[i] = jnp.concatenate([m_ref[i, :, k * pad : (k + 1) * pad] for k in range(3)], axis=0).T
+        y_ref[i] = jnp.dot(left[i % 2], xs[i], preferred_element_type=jnp.float32)[:seg]
 
     @pl.loop(0, pairs)
     def _(p):
@@ -326,6 +330,7 @@
             pltpu.VMEM((2, lay.tall, 3 * pad), bf16),
             pltpu.VMEM((4, rows, pad), f32),
             pltpu.VMEM((rows, 2 * pad), f32),
+            pltpu.VMEM((rows, pad, 6 * lay.count), bf16),
             pltpu.SemaphoreType.DMA((4,)),
             pltpu.SemaphoreType.DMA((rows // 2,)),
             pltpu.SemaphoreType.DMA((ring - 1, rows // 2)),

time: 16.5 us -> 16.4 us (level)
  no operation moved by 1% of the time
where the time goes in v8:
time: 16.4 us; the launch traced here: 16.2 us
  Pallas kernels  14.1 us (86%)
  local copies, waits for them, and re-layouts  2.09 us (13%)
    pallas_call x1, Pallas kernels, local(): pl.pallas_call(functools.partial(filter_kernel, lay, bands, top), out_sha...  14.1 us
    unnamed x1, local copies, waits for them, and re-layouts  2.09 us

profile of v8, /device:TPU:0, one launch (start us, length us, event | category | flops | bytes accessed | tf_op | source)
XLA Modules:
  0.0 16.2 jit_solution(5694994900741136009)
XLA Ops:
  0.0 14.1 %filter.1 = f32[8,360,384]{2,1,0:T(8,128)S(1)} custom-call(s32[8]{0:T(128)} %cut_hbm.1, f32[8,360,384]{2,1,0:T(8,128)} %x_hbm.1, f32[107,24,128]{2,1,0:T(8,128)} %constant.6.clone.line_hbm, f32[214,24,128]{2,1,0:T(8,128)} %constant.7.clone.mix_hbm, f32[2,16,384]{2,1,0:T(8,128)} %constant.8.clone.bank_hbm), custom_call_target="tpu_custom_call" | custom-call | tf_op jit(solution)/shard_map/filter/pallas_call | solution.py:315
  14.1 2.1 %copy.7 = f32[8,360,384]{2,1,0:T(8,128)} copy(f32[8,360,384]{2,1,0:T(8,128)S(1)} %filter.1) | data formatting | bytes 8847360

commit v9 on v8

--- a/solution.py
+++ b/solution.py
@@ -129,7 +129,7 @@
     return hi, mid, (rest - mid.astype(jnp.float32)).astype(jnp.bfloat16)
 
 
-def filter_kernel(lay, bands, top, cut_hbm, x_hbm, line_hbm, mix_hbm, bank_hbm, y_ref, cut_ref, x_ref, line_ref, mix_ref, bank_ref, come_ref, m_ref, send, xs, left, turns, both, mt_ref, load_sem, x_sem, send_sem, recv_sem):
+def filter_kernel(lay, bands, top, cut_hbm, x_hbm, line_hbm, mix_hbm, bank_hbm, y_ref, cut_ref, x_ref, line_ref, mix_ref, bank_ref, come_ref, m_ref, send, xs, left, turns, both, mt_ref, load_sem, mix_sem, x_sem, send_sem, recv_sem):
     seg, pad, ring, pairs = lay.segment, lay.padded, lay.ring, lay.rows // 2
     length = seg * ring
     band, me = lax.axis_index("lat"), lax.axis_index("lon")
@@ -155,11 +155,16 @@
 
     loads = [
         pltpu.make_async_copy(a, b, load_sem.at[k])
-        for k, (a, b) in enumerate(((cut_hbm, cut_ref), (bank_hbm, bank_ref), (mix_hbm, mix_ref), (line_hbm, line_ref)))
+        for k, (a, b) in enumerate(((cut_hbm, cut_ref), (bank_hbm, bank_ref), (line_hbm, line_ref)))
     ]
-    for copy in loads[:3]:
+    groups = mix_hbm.shape[0]
+    cuts_at = [groups * k // 4 for k in range(5)]
+    mixes = [
+        pltpu.make_async_copy(mix_hbm.at[pl.ds(a, b - a)], mix_ref.at[pl.ds(a, b - a)], mix_sem.at[k])
+        for k, (a, b) in enumerate(zip(cuts_at, cuts_at[1:]))
+    ]
+    for copy in loads[:2] + mixes + [fetch(0)]:
         copy.start()
-    fetch(0).start()
     for step in range(1, ring):
         pl.semaphore_signal(barrier, inc=1, device_id={"lon": lax.rem(me + step, ring)}, device_id_type=MESH)
 
@@ -168,7 +173,7 @@
             for k in range(3):
                 xs[r, k * pad + seg : (k + 1) * pad] = jnp.zeros((pad - seg, lay.channels), jnp.bfloat16)
     loads[0].wait()
-    for copy in [fetch(1), loads[3]] + [fetch(p) for p in range(2, pairs)]:
+    for copy in [fetch(p) for p in range(1, pairs)] + [loads[2]]:
         copy.start()
     row = lax.broadcasted_iota(jnp.int32, (lay.rows, pad), 0)
     spot = lax.broadcasted_iota(jnp.int32, (lay.rows, pad), 1).astype(jnp.float32)
@@ -183,7 +188,8 @@
         turns[2 * f + 1] = jnp.sin(angle)
     slot = lax.broadcasted_iota(jnp.int32, (lay.count, LANES), 1)
     loads[1].wait()
-    loads[2].wait()
+    for copy in mixes:
+        copy.wait()
 
     def mixed(i):
         x = x_ref[i]
@@ -274,7 +280,7 @@
         for n in range(ring - 1):
             push(n, p).start()
 
-    loads[3].wait()
+    loads[2].wait()
     mirror()
 
     for i in range(lay.rows):
@@ -331,6 +337,7 @@
             pltpu.VMEM((4, rows, pad), f32),
             pltpu.VMEM((rows, 2 * pad), f32),
             pltpu.VMEM((rows, pad, 6 * lay.count), bf16),
+            pltpu.SemaphoreType.DMA((3,)),
             pltpu.SemaphoreType.DMA((4,)),
             pltpu.SemaphoreType.DMA((rows // 2,)),
             pltpu.SemaphoreType.DMA((ring - 1, rows // 2)),

time: 16.4 us -> 16.4 us (level)
  no operation moved by 1% of the time
where the time goes in v9:
time: 16.4 us; the launch traced here: 16.2 us
  Pallas kernels  14.1 us (86%)
  local copies, waits for them, and re-layouts  2.09 us (13%)
    pallas_call x1, Pallas kernels, local(): pl.pallas_call(functools.partial(filter_kernel, lay, bands, top), out_sha...  14.1 us
    unnamed x1, local copies, waits for them, and re-layouts  2.09 us

profile of v9, /device:TPU:0, one launch (start us, length us, event | category | flops | bytes accessed | tf_op | source)
XLA Modules:
  0.0 16.2 jit_solution(4541883323790168521)
XLA Ops:
  0.0 14.1 %filter.1 = f32[8,360,384]{2,1,0:T(8,128)S(1)} custom-call(s32[8]{0:T(128)} %cut_hbm.1, f32[8,360,384]{2,1,0:T(8,128)} %x_hbm.1, f32[107,24,128]{2,1,0:T(8,128)} %constant.6.clone.line_hbm, f32[214,24,128]{2,1,0:T(8,128)} %constant.7.clone.mix_hbm, f32[2,16,384]{2,1,0:T(8,128)} %constant.8.clone.bank_hbm), custom_call_target="tpu_custom_call" | custom-call | tf_op jit(solution)/shard_map/filter/pallas_call | solution.py:321
  14.2 2.1 %copy.7 = f32[8,360,384]{2,1,0:T(8,128)} copy(f32[8,360,384]{2,1,0:T(8,128)S(1)} %filter.1) | data formatting | bytes 8847360
